TPU v7x, 32 devices: a whole 2x2x4 slice. The times are simulated.
32 devices in a mesh: ctx: 8 (over z, core), fsdp: 4 (over y, x).
Axes of the slice: x: 2, y: 2, z: 4, core: 2. Of those that a mesh axis runs over, the one named last changes fastest.
Arguments:
- inputs: float32 [4096, 2048], P(('ctx', 'fsdp')), may hold values from -6 to 6
- cotangent: float32 [4096, 2048], P(('ctx', 'fsdp')), may hold values from -6 to 6
- positions: int32 [4096], replicated, may hold values from 0 to 4095, as said below
- gain_attention: float32 [2048], P('ctx'), may hold values from 0.9 to 1.1
- shift_attention: float32 [2048], P('ctx'), may hold values from -0.18 to 0.18
- weight_project: float32 [2048, 3, 2048], P('ctx', None, 'fsdp'), may hold values from -0.1875 to 0.1875
- bias_project: float32 [3, 32, 64], P(None, 'fsdp', 'ctx'), may hold values from -0.18 to 0.18
- weight_output: float32 [2048, 2048], P('fsdp', 'ctx'), may hold values from -0.75 to 0.75
- gain_feedforward: float32 [2048], P('ctx'), may hold values from 0.1 to 1.9
- shift_feedforward: float32 [2048], P('ctx'), may hold values from -0.18 to 0.18
- weight_gateup: float32 [2048, 2, 5632], P('ctx', None, 'fsdp'), may hold values from -0.125 to 0.125
- weight_down: float32 [5632, 2048], P('fsdp', 'ctx'), may hold values from -0.078125 to 0.078125
- momentum_gain_attention: float32 [2048], P('ctx'), may hold values from -20 to 20
- momentum_shift_attention: float32 [2048], P('ctx'), may hold values from -20 to 20
- momentum_weight_project: float32 [2048, 3, 2048], P('ctx', None, 'fsdp'), may hold values from -20 to 20
- momentum_bias_project: float32 [3, 32, 64], P(None, 'fsdp', 'ctx'), may hold values from -20 to 20
- momentum_weight_output: float32 [2048, 2048], P('fsdp', 'ctx'), may hold values from -20 to 20
- momentum_gain_feedforward: float32 [2048], P('ctx'), may hold values from -20 to 20
- momentum_shift_feedforward: float32 [2048], P('ctx'), may hold values from -20 to 20
- momentum_weight_gateup: float32 [2048, 2, 5632], P('ctx', None, 'fsdp'), may hold values from -20 to 20
- momentum_weight_down: float32 [5632, 2048], P('fsdp', 'ctx'), may hold values from -20 to 20
- variance_gain_attention: float32 [2048], P('ctx'), may hold values from 409.6 to 1638.4
- variance_shift_attention: float32 [2048], P('ctx'), may hold values from 409.6 to 1638.4
- variance_weight_project: float32 [2048, 3, 2048], P('ctx', None, 'fsdp'), may hold values from 40.96 to 163.84
- variance_bias_project: float32 [3, 32, 64], P(None, 'fsdp', 'ctx'), may hold values from 40.96 to 163.84
- variance_weight_output: float32 [2048, 2048], P('fsdp', 'ctx'), may hold values from 40.96 to 163.84
- variance_gain_feedforward: float32 [2048], P('ctx'), may hold values from 40.96 to 163.84
- variance_shift_feedforward: float32 [2048], P('ctx'), may hold values from 40.96 to 163.84
- variance_weight_gateup: float32 [2048, 2, 5632], P('ctx', None, 'fsdp'), may hold values from 40.96 to 163.84
- variance_weight_down: float32 [5632, 2048], P('fsdp', 'ctx'), may hold values from 40.96 to 163.84
Outputs:
- output: float32 [4096, 2048], P(('ctx', 'fsdp'))
- input_grad: float32 [4096, 2048], P(('ctx', 'fsdp'))
- gradient_gain_attention: float32 [2048], P('ctx')
- gradient_shift_attention: float32 [2048], P('ctx')
- gradient_weight_project: float32 [2048, 3, 2048], P('ctx', None, 'fsdp')
- gradient_bias_project: float32 [3, 32, 64], P(None, 'fsdp', 'ctx')
- gradient_weight_output: float32 [2048, 2048], P('fsdp', 'ctx')
- gradient_gain_feedforward: float32 [2048], P('ctx')
- gradient_shift_feedforward: float32 [2048], P('ctx')
- gradient_weight_gateup: float32 [2048, 2, 5632], P('ctx', None, 'fsdp')
- gradient_weight_down: float32 [5632, 2048], P('fsdp', 'ctx')
- update_gain_attention: float32 [2048], P('ctx')
- new_shift_attention: float32 [2048], P('ctx')
- new_weight_project: float32 [2048, 3, 2048], P('ctx', None, 'fsdp')
- new_bias_project: float32 [3, 32, 64], P(None, 'fsdp', 'ctx')
- new_weight_output: float32 [2048, 2048], P('fsdp', 'ctx')
- update_gain_feedforward: float32 [2048], P('ctx')
- new_shift_feedforward: float32 [2048], P('ctx')
- new_weight_gateup: float32 [2048, 2, 5632], P('ctx', None, 'fsdp')
- new_weight_down: float32 [5632, 2048], P('fsdp', 'ctx')
- next_momentum_gain_attention: float32 [2048], P('ctx')
- next_momentum_shift_attention: float32 [2048], P('ctx')
- next_momentum_weight_project: float32 [2048, 3, 2048], P('ctx', None, 'fsdp')
- next_momentum_bias_project: float32 [3, 32, 64], P(None, 'fsdp', 'ctx')
- next_momentum_weight_output: float32 [2048, 2048], P('fsdp', 'ctx')
- next_momentum_gain_feedforward: float32 [2048], P('ctx')
- next_momentum_shift_feedforward: float32 [2048], P('ctx')
- next_momentum_weight_gateup: float32 [2048, 2, 5632], P('ctx', None, 'fsdp')
- next_momentum_weight_down: float32 [5632, 2048], P('fsdp', 'ctx')
- next_variance_gain_attention: float32 [2048], P('ctx')
- next_variance_shift_attention: float32 [2048], P('ctx')
- next_variance_weight_project: float32 [2048, 3, 2048], P('ctx', None, 'fsdp')
- next_variance_bias_project: float32 [3, 32, 64], P(None, 'fsdp', 'ctx')
- next_variance_weight_output: float32 [2048, 2048], P('fsdp', 'ctx')
- next_variance_gain_feedforward: float32 [2048], P('ctx')
- next_variance_shift_feedforward: float32 [2048], P('ctx')
- next_variance_weight_gateup: float32 [2048, 2, 5632], P('ctx', None, 'fsdp')
- next_variance_weight_down: float32 [5632, 2048], P('fsdp', 'ctx')
Inputs may be any that keep to these rules, and one draw needn't show every extreme that they name: positions holds each of 0 to 4095 once. Rows fall in aligned runs of 256, each holding one block of 256 consecutive positions in rising order, and the two runs of each aligned run of 512 rows hold block j and block 15 - j for some j.
All inputs are finite; a program needn't handle non-finite values.
Results may differ from a plain program's by a relative error of at most 0.025.
Values may be sent and summed in bfloat16 or wider, within the bound.
A program may use at most 160 MiB of HBM per device.

v0:
```python
from functools import partial
import math

import jax
import jax.numpy as jnp
from jax import lax
from jax.sharding import PartitionSpec as P

D = 2048
H = 32
HD = 64
ROT = 16


norm_eps = 1e-05
rope_base = 10000.0
masked_score = -1e30
learn_rate = 0.1
beta_one = 0.9
beta_two = 0.95
adam_eps = 1e-08
decay_rate = 0.1
adam_step = 10


def norm_parts(values):
    center = values - jnp.mean(values, axis=-1, keepdims=True)
    inverse = lax.rsqrt(jnp.mean(center * center, axis=-1, keepdims=True) + norm_eps)
    return (center * inverse, inverse)


def norm_back(grad_out, normed, inverse, gain_vector):
    scaled = grad_out * gain_vector
    inner_mean = jnp.mean(scaled * normed, axis=-1, keepdims=True)
    return (scaled - jnp.mean(scaled, axis=-1, keepdims=True) - normed * inner_mean) * inverse


def rotary_tables(where_at):
    half_dims = ROT // 2
    frequency = rope_base ** (-(jnp.arange(half_dims, dtype=jnp.float32) * 2.0) / ROT)
    angles = where_at.astype(jnp.float32)[:, None] * frequency[None, :]
    return (jnp.cos(angles)[:, None, :], jnp.sin(angles)[:, None, :])


def rotate(head_values, where_at):
    cosine, sine_part = rotary_tables(where_at)
    half_dims = ROT // 2
    first_half = head_values[..., :half_dims]
    second = head_values[..., half_dims:ROT]
    return jnp.concatenate(
        [
            first_half * cosine - second * sine_part,
            second * cosine + first_half * sine_part,
            head_values[..., ROT:],
        ],
        axis=-1,
    )


def unrotate(head_grads, where_at):
    cosine, sine_part = rotary_tables(where_at)
    half_dims = ROT // 2
    first_half = head_grads[..., :half_dims]
    second = head_grads[..., half_dims:ROT]
    return jnp.concatenate(
        [
            first_half * cosine + second * sine_part,
            second * cosine - first_half * sine_part,
            head_grads[..., ROT:],
        ],
        axis=-1,
    )


def rounded_float(values):
    return lax.optimization_barrier(values.astype(jnp.bfloat16)).astype(jnp.float32)


def keep_state(state_now):
    return state_now


def masked_scores(query_block, key_block, query_pos, key_pos):
    scores = jnp.einsum(
        "qhd,khd->hqk", query_block, key_block, preferred_element_type=jnp.float32
    ) * HD ** (-0.5)
    allowed = (query_pos[:, None] >= key_pos[None, :])[None]
    return (scores, allowed)


def attend_block(query_block, query_pos, key_sub, value_sub, pos_sub, state_now):
    row_top, row_total, weighted = state_now
    scores, allowed = masked_scores(query_block, key_sub, query_pos, pos_sub)
    scores = jnp.where(allowed, scores, masked_score)
    new_top = jnp.maximum(row_top, jnp.max(scores, axis=-1))
    weights = jnp.where(allowed, jnp.exp(scores - new_top[..., None]), 0.0)
    factor = jnp.exp(row_top - new_top)
    mixed_block = jnp.einsum(
        "hqk,khd->hqd", weights.astype(jnp.bfloat16), value_sub, preferred_element_type=jnp.float32
    )
    return (
        new_top,
        row_total * factor + jnp.sum(weights, axis=-1),
        weighted * factor[..., None] + mixed_block,
    )


def back_block(
    query_block, query_pos, grad_block, lse_half, delta_half, key_sub, value_sub, pos_sub, state_now
):
    query_grad, key_grad, value_grad = state_now
    scores, allowed = masked_scores(query_block, key_sub, query_pos, pos_sub)
    weights = jnp.where(allowed, jnp.exp(scores - lse_half[..., None]), 0.0)
    value_grad = value_grad + jnp.einsum(
        "hqk,qhd->khd", weights.astype(jnp.bfloat16), grad_block, preferred_element_type=jnp.float32
    )
    weight_grads = jnp.einsum(
        "qhd,khd->hqk", grad_block, value_sub, preferred_element_type=jnp.float32
    )
    score_grads = (weights * (weight_grads - delta_half[..., None])).astype(jnp.bfloat16)
    query_grad = query_grad + jnp.einsum(
        "hqk,khd->hqd", score_grads, key_sub, preferred_element_type=jnp.float32
    ) * HD ** (-0.5)
    key_grad = key_grad + jnp.einsum(
        "hqk,qhd->khd", score_grads, query_block, preferred_element_type=jnp.float32
    ) * HD ** (-0.5)
    return (query_grad, key_grad, value_grad)


def piece_layout(shard_piece, pos_all, row_count):
    key_piece, value_piece = shard_piece
    piece_rows = key_piece.shape[0]
    block_rows = math.gcd(piece_rows, row_count)
    block_count = piece_rows // block_rows
    key_pos = pos_all.reshape(block_count, block_rows)
    key_blocks = key_piece.reshape(block_count, block_rows, -1, HD)
    value_blocks = value_piece.reshape(block_count, block_rows, -1, HD)
    return (block_rows, block_count, key_pos, key_blocks, value_blocks)


def query_side_fold(block_fns, pos_halves, pos_all, row_count, states, shard_piece):
    block_rows, block_count, key_pos, key_blocks, value_blocks = piece_layout(
        shard_piece, pos_all, row_count
    )
    sub_rows = block_rows // 2

    def query_scan_step(carried, block_item):
        key_block, value_block, block_pos = block_item
        current = [carried[0], carried[1]]
        for key_half in range(2):
            key_sub = key_block[key_half * sub_rows : (key_half + 1) * sub_rows]
            value_sub = value_block[key_half * sub_rows : (key_half + 1) * sub_rows]
            pos_sub = block_pos[key_half * sub_rows : (key_half + 1) * sub_rows]
            for which_half in range(2):
                needed = jnp.min(pos_sub) <= jnp.max(pos_halves[which_half])
                current[which_half] = lax.cond(
                    needed,
                    partial(block_fns[which_half], key_sub, value_sub, pos_sub),
                    keep_state,
                    current[which_half],
                )
        return ((current[0], current[1]), None)

    states, unused = lax.scan(query_scan_step, states, (key_blocks, value_blocks, key_pos))
    return states


def backward_fold(
    query_halves,
    pos_halves,
    grad_halves,
    lse_halves,
    delta_halves,
    pos_all,
    row_count,
    states,
    shard_piece,
):
    block_rows, block_count, key_pos, key_blocks, value_blocks = piece_layout(
        shard_piece, pos_all, row_count
    )
    sub_rows = block_rows // 2
    offsets = jnp.arange(block_count, dtype=jnp.int32) * block_rows

    def backward_scan_step(carried, block_item):
        query_grads, key_grads, value_grads = carried
        key_block, value_block, block_pos, offset = block_item
        current = [query_grads[0], query_grads[1]]
        key_parts = []
        value_parts = []
        for key_half in range(2):
            key_sub = key_block[key_half * sub_rows : (key_half + 1) * sub_rows]
            value_sub = value_block[key_half * sub_rows : (key_half + 1) * sub_rows]
            pos_sub = block_pos[key_half * sub_rows : (key_half + 1) * sub_rows]
            key_acc = jnp.zeros((sub_rows, key_block.shape[1], HD), jnp.float32)
            value_acc = jnp.zeros((sub_rows, key_block.shape[1], HD), jnp.float32)
            for which_half in range(2):
                needed = jnp.min(pos_sub) <= jnp.max(pos_halves[which_half])
                current[which_half], key_acc, value_acc = lax.cond(
                    needed,
                    partial(
                        back_block,
                        query_halves[which_half],
                        pos_halves[which_half],
                        grad_halves[which_half],
                        lse_halves[which_half],
                        delta_halves[which_half],
                        key_sub,
                        value_sub,
                        pos_sub,
                    ),
                    keep_state,
                    (current[which_half], key_acc, value_acc),
                )
            key_parts.append(key_acc)
            value_parts.append(value_acc)
        key_grads = lax.dynamic_update_slice_in_dim(
            key_grads, jnp.concatenate(key_parts, axis=0).reshape(block_rows, -1), offset, 0
        )
        value_grads = lax.dynamic_update_slice_in_dim(
            value_grads, jnp.concatenate(value_parts, axis=0).reshape(block_rows, -1), offset, 0
        )
        return (((current[0], current[1]), key_grads, value_grads), None)

    states, unused = lax.scan(
        backward_scan_step, states, (key_blocks, value_blocks, key_pos, offsets)
    )
    return states


def adam_update(param, grad_value, moment_old, second_old):
    moment = beta_one * moment_old + (1.0 - beta_one) * grad_value
    second_moment = beta_two * second_old + (1.0 - beta_two) * grad_value * grad_value
    corrected = moment / (1.0 - beta_one**adam_step)
    root_term = jnp.sqrt(second_moment / (1.0 - beta_two**adam_step)) + adam_eps
    return (
        param - learn_rate * (corrected / root_term + decay_rate * param),
        moment,
        second_moment,
    )


def local(
    inputs,
    cotangent,
    positions,
    gain_attention,
    shift_attention,
    weight_project,
    bias_project,
    weight_output,
    gain_feedforward,
    shift_feedforward,
    weight_gateup,
    weight_down,
    momentum_gain_attention,
    momentum_shift_attention,
    momentum_weight_project,
    momentum_bias_project,
    momentum_weight_output,
    momentum_gain_feedforward,
    momentum_shift_feedforward,
    momentum_weight_gateup,
    momentum_weight_down,
    variance_gain_attention,
    variance_shift_attention,
    variance_weight_project,
    variance_bias_project,
    variance_weight_output,
    variance_gain_feedforward,
    variance_shift_feedforward,
    variance_weight_gateup,
    variance_weight_down,
):
    tokens = inputs.shape[0]
    groups = lax.axis_size("fsdp")
    contexts = lax.axis_size("ctx")
    heads_here = H // groups
    width_here = heads_here * HD
    row_count = tokens * groups
    half_rows = row_count // 2
    total_keys = row_count * contexts
    row_pos = lax.dynamic_slice_in_dim(positions, lax.axis_index("ctx") * row_count, row_count)
    own_start = lax.axis_index("fsdp") * tokens
    pos_halves = (row_pos[:half_rows], row_pos[half_rows:])
    (
        gain_one,
        shift_one,
        group_project,
        group_bias,
        group_output,
        gain_two,
        shift_two,
        group_gateup,
        group_down,
    ) = (
        lax.all_gather(gain_attention.astype(jnp.bfloat16), "ctx", axis=0, tiled=True),
        lax.all_gather(shift_attention.astype(jnp.bfloat16), "ctx", axis=0, tiled=True),
        lax.all_gather(weight_project.astype(jnp.bfloat16), "ctx", axis=0, tiled=True),
        lax.all_gather(bias_project.astype(jnp.bfloat16), "ctx", axis=2, tiled=True),
        lax.all_gather(weight_output.astype(jnp.bfloat16), "ctx", axis=1, tiled=True),
        lax.all_gather(gain_feedforward.astype(jnp.bfloat16), "ctx", axis=0, tiled=True),
        lax.all_gather(shift_feedforward.astype(jnp.bfloat16), "ctx", axis=0, tiled=True),
        lax.all_gather(weight_gateup.astype(jnp.bfloat16), "ctx", axis=0, tiled=True),
        lax.all_gather(weight_down.astype(jnp.bfloat16), "ctx", axis=1, tiled=True),
    )
    group_inputs, group_cotangent = (
        lax.all_gather(inputs, "fsdp", axis=0, tiled=True),
        lax.all_gather(cotangent, "fsdp", axis=0, tiled=True),
    )
    normed_one, inverse_one = norm_parts(group_inputs)
    first_act = (normed_one * gain_one.astype(jnp.float32) + shift_one.astype(jnp.float32)).astype(
        jnp.bfloat16
    )
    projected = jnp.dot(
        first_act, group_project.reshape(D, 3 * width_here), preferred_element_type=jnp.float32
    ) + group_bias.reshape(3 * width_here).astype(jnp.float32)
    split_cols = projected.reshape(row_count, 3, heads_here, HD)
    query_heads = rotate(split_cols[:, 0], row_pos).astype(jnp.bfloat16)
    head_key = rotate(split_cols[:, 1], row_pos).reshape(row_count, width_here).astype(jnp.bfloat16)
    head_value = split_cols[:, 2].reshape(row_count, width_here).astype(jnp.bfloat16)
    query_halves = (query_heads[:half_rows], query_heads[half_rows:])
    start_state = (
        jnp.full((heads_here, half_rows), masked_score, jnp.float32),
        jnp.zeros((heads_here, half_rows), jnp.float32),
        jnp.zeros((heads_here, half_rows, HD), jnp.float32),
    )
    attend_fns = (
        partial(attend_block, query_halves[0], pos_halves[0]),
        partial(attend_block, query_halves[1], pos_halves[1]),
    )
    states = query_side_fold(
        attend_fns,
        pos_halves,
        positions,
        row_count,
        (start_state, start_state),
        (
            lax.all_gather(head_key, "ctx", axis=0, tiled=True),
            lax.all_gather(head_value, "ctx", axis=0, tiled=True),
        ),
    )
    lse_halves = (states[0][0] + jnp.log(states[0][1]), states[1][0] + jnp.log(states[1][1]))
    attended = jnp.concatenate(
        [states[0][2] / states[0][1][..., None], states[1][2] / states[1][1][..., None]], axis=1
    )
    mixed_heads = (
        jnp.transpose(attended, (1, 0, 2)).reshape(row_count, width_here).astype(jnp.bfloat16)
    )
    middle = group_inputs + lax.psum(
        jnp.dot(mixed_heads, group_output, preferred_element_type=jnp.float32), "fsdp"
    )
    normed_two, inverse_two = norm_parts(middle)
    second_act = (normed_two * gain_two.astype(jnp.float32) + shift_two.astype(jnp.float32)).astype(
        jnp.bfloat16
    )
    gate_up = jnp.einsum(
        "td,dgu->tgu", second_act, group_gateup, preferred_element_type=jnp.float32
    )
    gate_part = gate_up[:, 0]
    up_part = gate_up[:, 1]
    hidden = (jax.nn.silu(gate_part) * up_part).astype(jnp.bfloat16)
    output_rows = middle + lax.psum(
        jnp.dot(hidden, group_down, preferred_element_type=jnp.float32), "fsdp"
    )
    output = lax.dynamic_slice_in_dim(output_rows, own_start, tokens)
    back_gain_one, back_project, back_output, back_gain_two, back_gateup, back_down = (
        lax.all_gather(gain_attention.astype(jnp.bfloat16), "ctx", axis=0, tiled=True),
        lax.all_gather(weight_project.astype(jnp.bfloat16), "ctx", axis=0, tiled=True),
        lax.all_gather(weight_output.astype(jnp.bfloat16), "ctx", axis=1, tiled=True),
        lax.all_gather(gain_feedforward.astype(jnp.bfloat16), "ctx", axis=0, tiled=True),
        lax.all_gather(weight_gateup.astype(jnp.bfloat16), "ctx", axis=0, tiled=True),
        lax.all_gather(weight_down.astype(jnp.bfloat16), "ctx", axis=1, tiled=True),
    )
    d_branch = group_cotangent.astype(jnp.bfloat16)
    grad_down = jnp.einsum("tu,td->ud", hidden, d_branch, preferred_element_type=jnp.float32)
    d_hidden = jnp.einsum("td,ud->tu", d_branch, back_down, preferred_element_type=jnp.float32)
    gate_sigmoid = jax.nn.sigmoid(gate_part)
    d_gate = d_hidden * up_part * gate_sigmoid * (1.0 + gate_part * (1.0 - gate_sigmoid))
    d_up = d_hidden * jax.nn.silu(gate_part)
    d_gate_up = jnp.stack([d_gate, d_up], axis=1).astype(jnp.bfloat16)
    grad_gateup = jnp.einsum(
        "td,tgu->dgu", second_act, d_gate_up, preferred_element_type=jnp.float32
    )
    d_second = lax.psum(
        jnp.einsum("tgu,dgu->td", d_gate_up, back_gateup, preferred_element_type=jnp.float32),
        "fsdp",
    )
    grad_gain_two = jnp.sum(d_second * normed_two, axis=0)
    grad_shift_two = jnp.sum(d_second, axis=0)
    d_middle = group_cotangent + norm_back(
        d_second, normed_two, inverse_two, back_gain_two.astype(jnp.float32)
    )
    d_attend = d_middle.astype(jnp.bfloat16)
    grad_output = jnp.einsum("te,td->ed", mixed_heads, d_attend, preferred_element_type=jnp.float32)
    d_mixed = jnp.einsum(
        "td,ed->te", d_attend, back_output, preferred_element_type=jnp.float32
    ).astype(jnp.bfloat16)
    grad_heads = d_mixed.reshape(row_count, heads_here, HD)
    row_delta = jnp.sum(
        jnp.transpose(grad_heads.astype(jnp.float32), (1, 0, 2)) * attended, axis=-1
    )
    grad_halves = (grad_heads[:half_rows], grad_heads[half_rows:])
    delta_halves = (row_delta[:, :half_rows], row_delta[:, half_rows:])
    zero_query = jnp.zeros((heads_here, half_rows, HD), jnp.float32)
    zero_keys = jnp.zeros((total_keys, width_here), jnp.float32)
    query_grads, key_grads, value_grads = backward_fold(
        query_halves,
        pos_halves,
        grad_halves,
        lse_halves,
        delta_halves,
        positions,
        row_count,
        ((zero_query, zero_query), zero_keys, zero_keys),
        (
            lax.all_gather(head_key, "ctx", axis=0, tiled=True),
            lax.all_gather(head_value, "ctx", axis=0, tiled=True),
        ),
    )
    summed_keys, summed_values = (
        lax.psum_scatter(key_grads, "ctx", scatter_dimension=0, tiled=True),
        lax.psum_scatter(value_grads, "ctx", scatter_dimension=0, tiled=True),
    )
    query_rows = jnp.transpose(jnp.concatenate([query_grads[0], query_grads[1]], axis=1), (1, 0, 2))
    query_back = unrotate(rounded_float(query_rows), row_pos)
    key_back = unrotate(rounded_float(summed_keys.reshape(row_count, heads_here, HD)), row_pos)
    value_back = (
        summed_values.reshape(row_count, heads_here, HD).astype(jnp.bfloat16).astype(jnp.float32)
    )
    d_projected = jnp.stack([query_back, key_back, value_back], axis=1).astype(jnp.bfloat16)
    grad_bias = jnp.sum(d_projected.astype(jnp.float32), axis=0)
    d_flat = d_projected.reshape(row_count, 3 * width_here)
    grad_project = jnp.einsum(
        "td,te->de", first_act, d_flat, preferred_element_type=jnp.float32
    ).reshape(D, 3, width_here)
    d_first = lax.psum(
        jnp.einsum(
            "te,de->td",
            d_flat,
            back_project.reshape(D, 3 * width_here),
            preferred_element_type=jnp.float32,
        ),
        "fsdp",
    )
    grad_gain_one = jnp.sum(d_first * normed_one, axis=0)
    grad_shift_one = jnp.sum(d_first, axis=0)
    input_rows = d_middle + norm_back(
        d_first, normed_one, inverse_one, back_gain_one.astype(jnp.float32)
    )
    input_grad = lax.dynamic_slice_in_dim(input_rows, own_start, tokens)
    gradients = list(
        (
            lax.psum_scatter(grad_gain_one, "ctx", scatter_dimension=0, tiled=True),
            lax.psum_scatter(grad_shift_one, "ctx", scatter_dimension=0, tiled=True),
            lax.psum_scatter(grad_project, "ctx", scatter_dimension=0, tiled=True),
            lax.psum_scatter(grad_bias, "ctx", scatter_dimension=2, tiled=True),
            lax.psum_scatter(grad_output, "ctx", scatter_dimension=1, tiled=True),
            lax.psum_scatter(grad_gain_two, "ctx", scatter_dimension=0, tiled=True),
            lax.psum_scatter(grad_shift_two, "ctx", scatter_dimension=0, tiled=True),
            lax.psum_scatter(grad_gateup, "ctx", scatter_dimension=0, tiled=True),
            lax.psum_scatter(grad_down, "ctx", scatter_dimension=1, tiled=True),
        )
    )
    params = [
        gain_attention,
        shift_attention,
        weight_project,
        bias_project,
        weight_output,
        gain_feedforward,
        shift_feedforward,
        weight_gateup,
        weight_down,
    ]
    momenta = [
        momentum_gain_attention,
        momentum_shift_attention,
        momentum_weight_project,
        momentum_bias_project,
        momentum_weight_output,
        momentum_gain_feedforward,
        momentum_shift_feedforward,
        momentum_weight_gateup,
        momentum_weight_down,
    ]
    variances = [
        variance_gain_attention,
        variance_shift_attention,
        variance_weight_project,
        variance_bias_project,
        variance_weight_output,
        variance_gain_feedforward,
        variance_shift_feedforward,
        variance_weight_gateup,
        variance_weight_down,
    ]
    new_params = []
    new_momenta = []
    new_variances = []
    for index in range(9):
        new_value, moment, second_moment = adam_update(
            params[index], gradients[index], momenta[index], variances[index]
        )
        new_params.append(new_value)
        new_momenta.append(moment)
        new_variances.append(second_moment)
    new_params[0] = new_params[0] - params[0]
    new_params[5] = new_params[5] - params[5]
    return tuple([output, input_grad] + gradients + new_params + new_momenta + new_variances)


def solution(mesh):
    in_specs = (
        P(("ctx", "fsdp"), None),
        P(("ctx", "fsdp"), None),
        P(),
        P("ctx"),
        P("ctx"),
        P("ctx", None, "fsdp"),
        P(None, "fsdp", "ctx"),
        P("fsdp", "ctx"),
        P("ctx"),
        P("ctx"),
        P("ctx", None, "fsdp"),
        P("fsdp", "ctx"),
        P("ctx"),
        P("ctx"),
        P("ctx", None, "fsdp"),
        P(None, "fsdp", "ctx"),
        P("fsdp", "ctx"),
        P("ctx"),
        P("ctx"),
        P("ctx", None, "fsdp"),
        P("fsdp", "ctx"),
        P("ctx"),
        P("ctx"),
        P("ctx", None, "fsdp"),
        P(None, "fsdp", "ctx"),
        P("fsdp", "ctx"),
        P("ctx"),
        P("ctx"),
        P("ctx", None, "fsdp"),
        P("fsdp", "ctx"),
    )
    out_specs = (
        P(("ctx", "fsdp"), None),
        P(("ctx", "fsdp"), None),
        P("ctx"),
        P("ctx"),
        P("ctx", None, "fsdp"),
        P(None, "fsdp", "ctx"),
        P("fsdp", "ctx"),
        P("ctx"),
        P("ctx"),
        P("ctx", None, "fsdp"),
        P("fsdp", "ctx"),
        P("ctx"),
        P("ctx"),
        P("ctx", None, "fsdp"),
        P(None, "fsdp", "ctx"),
        P("fsdp", "ctx"),
        P("ctx"),
        P("ctx"),
        P("ctx", None, "fsdp"),
        P("fsdp", "ctx"),
        P("ctx"),
        P("ctx"),
        P("ctx", None, "fsdp"),
        P(None, "fsdp", "ctx"),
        P("fsdp", "ctx"),
        P("ctx"),
        P("ctx"),
        P("ctx", None, "fsdp"),
        P("fsdp", "ctx"),
        P("ctx"),
        P("ctx"),
        P("ctx", None, "fsdp"),
        P(None, "fsdp", "ctx"),
        P("fsdp", "ctx"),
        P("ctx"),
        P("ctx"),
        P("ctx", None, "fsdp"),
        P("fsdp", "ctx"),
    )
    return jax.shard_map(local, mesh=mesh, in_specs=in_specs, out_specs=out_specs, check_vma=False)
```

profile of v0, /device:TPU:0, one launch (start us, length us, event | category | flops | bytes accessed | tf_op | source)
XLA Modules:
  0.0 2026.2 jit_solution(16278181921438597005)
XLA Ops:
  10.8 15.7 all_gather.51
  26.7 11.8 all-gather.1
  38.5 8.8 all-gather
  47.5 17.7 all-gather.13.cloned.1.call-done
  73.6 59.0 %all-gather.15.cloned.1.call-done = bf16[2048,3,512]{0,2,1:T(8,128)(2,1)} async-done(((bf16[256,3,512]{0,2,1:T(8,128)(2,1)}), bf16[2048,3,512]{0,2,1:T(8,128)(2,1)}) %all-gather.15.cloned.1.call-update) | async-done | bytes 6291472 | tf_op jit(solution)/shard_map/all_gather | solution.py:299
  132.6 9.2 convolution_add_fusion.4
  152.1 41.3 %all-gather.17.cloned.1.call-done = bf16[4096,512]{0,1:T(8,128)(2,1)} async-done(((bf16[512,512]{0,1:T(8,128)(2,1)}), bf16[4096,512]{0,1:T(8,128)(2,1)}) %all-gather.17.cloned.1.call-update) | async-done | bytes 4194320 | tf_op jit(solution)/shard_map/all_gather | solution.py:339
  201.3 39.9 %all-gather.19.cloned.1.call-done = bf16[4096,512]{0,1:T(8,128)(2,1)} async-done(((bf16[512,512]{0,1:T(8,128)(2,1)}), bf16[4096,512]{0,1:T(8,128)(2,1)}) %all-gather.19.cloned.1.call-update) | async-done | bytes 4194320 | tf_op jit(solution)/shard_map/all_gather | solution.py:340
  249.2 91.2 %while.41 = (s32[]{:T(128)}, f32[8,256]{1,0:T(8,128)S(1)}, f32[8,256]{1,0:T(8,128)S(1)}, f32[8,256,64]{1,2,0:T(8,128)S(1)}, f32[8,256]{1,0:T(8,128)S(1)}, /*inde...) while((s32[]{:T(128)}, f32[8,256]{1,0:T(8,128)S(1)}, ...), condition=%wide.region_23.24_spmd, body=%wide.region_4.23_spmd.sunk | while | flops 565461504 | bytes 36188860 | solution.py:164
  351.5 9.6 all-gather.3
  361.1 9.3 all-gather.2
  370.4 77.9 %all-reduce.11.cloned.1.call-done = f32[512,2048]{1,0:T(8,128)} async-done(((f32[512,2048]{1,0:T(8,128)}), f32[512,2048]{1,0:T(8,128)}) %all-reduce.11.cloned.1.call-update) | async-done | bytes 4194320 | tf_op jit(solution)/shard_map/psum | solution.py:350
  454.3 104.2 %all-gather.23.cloned.1.call-done = bf16[2048,2,1408]{2,0,1:T(8,128)(2,1)} async-done(((bf16[256,2,1408]{2,0,1:T(8,128)(2,1)}), bf16[2048,2,1408]{2,0,1:T(8,128)(2,1)}) %all-gather.23.cloned.1.call-update) | async-done | bytes 11534352 | tf_op jit(solution)/shard_map/all_gather | solution.py:304
  558.5 13.5 fusion.92
  572.0 39.2 %all-gather.27.cloned.1.call-done = f32[512,2048]{1,0:T(8,128)} async-done(((f32[128,2048]{1,0:T(8,128)}), f32[512,2048]{1,0:T(8,128)}) %all-gather.27.cloned.1.call-update) | async-done | bytes 4194320 | tf_op jit(solution)/shard_map/all_gather | solution.py:309
  611.2 63.0 %all-gather.25.cloned.1.call-done = bf16[1408,2048]{1,0:T(8,128)(2,1)} async-done(((bf16[1408,256]{1,0:T(8,128)(2,1)}), bf16[1408,2048]{1,0:T(8,128)(2,1)}) %all-gather.25.cloned.1.call-update) | async-done | bytes 5767184 | tf_op jit(solution)/shard_map/all_gather | solution.py:305
  674.2 11.0 fusion.70
  686.8 10.4 convolution_bitcast_fusion.4
  697.9 101.3 %all-reduce.13.cloned.1.call-done = f32[512,2048]{1,0:T(8,128)} async-done(((f32[512,2048]{1,0:T(8,128)}), f32[512,2048]{1,0:T(8,128)}) %all-reduce.13.cloned.1.call-update) | async-done | bytes 4194320 | tf_op jit(solution)/shard_map/psum | solution.py:385
  821.4 293.9 %while.42 = (s32[]{:T(128)}, f32[8,256,64]{1,2,0:T(8,128)}, f32[8,256,64]{1,2,0:T(8,128)}, f32[4096,512]{0,1:T(8,128)}, f32[4096,512]{0,1:T(8,128)}, /*index=5*/...) while((s32[]{:T(128)}, f32[8,256,64]{1,2,0:T(8,128)}, ...), condition=%wide.region_43.44_spmd, body=%wide.region_32.43_spmd.sunk | while | flops 1359741440 | bytes 77247560 | solution.py:225
  827.7 6.2 conditional.20
  849.9 6.1 dynamic_update_slice.10
  857.2 6.1 dynamic_update_slice.11
  869.5 6.2 conditional.21
  886.1 6.1 dynamic_update_slice.10
  905.6 6.2 conditional.20
  923.7 6.1 dynamic_update_slice.10
  943.2 6.2 conditional.21
  959.8 6.1 dynamic_update_slice.10
  967.0 6.1 dynamic_update_slice.11
  979.4 6.2 conditional.21
  1015.5 6.2 conditional.21
  1032.1 6.1 dynamic_update_slice.10
  1039.4 6.1 dynamic_update_slice.11
  1074.9 6.1 dynamic_update_slice.11
  1123.3 10.0 fusion.78
  1133.3 7.7 fusion.117
  1142.3 73.8 %reduce-scatter.8.cloned.1.call-done = f32[512,512]{0,1:T(8,128)} async-done(((f32[4096,512]{0,1:T(8,128)}), f32[512,512]{0,1:T(8,128)}) %reduce-scatter.8.cloned.1.call-update) | async-done | bytes 1048592 | tf_op jit(solution)/shard_map/reduce_scatter | solution.py:422
  1217.6 88.7 %reduce-scatter.10.cloned.1.call-done = f32[512,512]{0,1:T(8,128)} async-done(((f32[4096,512]{0,1:T(8,128)}), f32[512,512]{0,1:T(8,128)}) %reduce-scatter.10.cloned.1.call-update) | async-done | bytes 1048592 | tf_op jit(solution)/shard_map/reduce_scatter | solution.py:423
  1308.8 7.8 fusion.118
  1317.3 13.6 fusion.66
  1331.6 8.9 fusion.64
  1343.2 14.4 reduce-scatter.14.cloned.1.call-done
  1360.0 118.0 %reduce-scatter.18.cloned.1.call-done = f32[1408,256]{1,0:T(8,128)} async-done(((f32[1408,2048]{1,0:T(8,128)}), f32[1408,256]{1,0:T(8,128)}) %reduce-scatter.18.cloned.1.call-update) | async-done | bytes 1441808 | tf_op jit(solution)/shard_map/reduce_scatter | solution.py:462
  1483.0 169.2 %all-reduce.15.cloned.1.call-done = (f32[512,2048]{1,0:T(8,128)}, f32[512,2048]{1,0:T(8,128)}) async-done(((f32[512,2048]{1,0:T(8,128)}, f32[512,2048]{1,0:T(8,128)}), (f32[512,2048]{1,0:T(8,128)}, f32[512,2048]{1,0:T(8,128)})) %all-reduce.15.cloned.1.call-update) | async-done | bytes 8388624 | tf_op jit(solution)/shard_map/psum | solution.py:363
  1658.2 31.2 %all-reduce.5 = (f32[2048]{0:T(1024)S(1)}, f32[2048]{0:T(1024)S(1)}, f32[3,8,64]{2,1,0:T(8,128)S(1)}, f32[2048]{0:T(1024)S(1)}, f32[2048]{0:T(1024)S(1)}) all-reduce(f32[2048]{0:T(1024)S(1)} %get-tuple-element.996, f32[2048]{0:T(1024)S(1)} %get-tuple-element.995, ...), channel_id=4, replica_groups=mesh['ctx'=8,'fsdp'=4] {'ctx'}, use_global_device_ids=true, to_apply=%region_50.51.clone | all-reduce | flops 9728 | bytes 77824
  1698.7 184.8 %reduce-scatter.16.cloned.1.call-done = f32[256,2,1408]{2,0,1:T(8,128)} async-done(((f32[2048,2,1408]{2,0,1:T(8,128)}), f32[256,2,1408]{2,0,1:T(8,128)}) %reduce-scatter.16.cloned.1.call-update) | async-done | bytes 2883600 | tf_op jit(solution)/shard_map/reduce_scatter | solution.py:461
  1904.6 109.4 %reduce-scatter.12.cloned.1.call-done = f32[256,3,512]{2,0,1:T(8,128)} async-done(((f32[2048,3,512]{2,0,1:T(8,128)}), f32[256,3,512]{2,0,1:T(8,128)}) %reduce-scatter.12.cloned.1.call-update) | async-done | bytes 1572880 | tf_op jit(solution)/shard_map/reduce_scatter | solution.py:456
  (759 shorter events, 457.1 us)
Async XLA Ops:
  7.2 31.2 %copy-start.62 = (f32[256]{0:T(256)S(1)}, f32[256]{0:T(256)}, u32[]{:S(2)}) copy-start(f32[256]{0:T(256)} %param.53) | copy-start | bytes 3076
  7.3 40.0 %copy-start.48 = (s32[4096]{0:T(1024)S(1)}, s32[4096]{0:T(1024)}, u32[]{:S(2)}) copy-start(s32[4096]{0:T(1024)} %param.52) | copy-start | bytes 49156
  7.3 58.0 %all-gather.13.cloned.1.call-start = ((), (), s32[]{:S(2)}) async-start(), calls=%async_computation.6 | async-start | bytes 5242880 | tf_op jit(solution)/shard_map/all_gather | solution.py:308
  8.0 124.6 %all-gather.15.cloned.1.call-start = ((), (), s32[]{:S(2)}) async-start(), calls=%async_computation.7 | async-start | bytes 7077888 | tf_op jit(solution)/shard_map/all_gather | solution.py:299
  10.6 182.8 %all-gather.17.cloned.1.call-start = ((), (), s32[]{:S(2)}) async-start(), calls=%async_computation.8 | async-start | bytes 4718592 | tf_op jit(solution)/shard_map/all_gather | solution.py:339
  38.5 94.1 %copy-start.58 = (f32[8,1,256]{2,1,0:T(1,128)}, f32[8,1,256]{2,1,0:T(1,128)S(1)}, u32[]{:S(2)}) copy-start(f32[8,1,256]{2,1,0:T(1,128)S(1)} %convert_element_type.271) | copy-start | bytes 24580
  47.3 85.3 %copy-start.40 = (f32[8,1,256]{2,1,0:T(1,128)}, f32[8,1,256]{2,1,0:T(1,128)S(1)}, u32[]{:S(2)}) copy-start(f32[8,1,256]{2,1,0:T(1,128)S(1)} %convert_element_type.270) | copy-start | bytes 24580
  47.5 99.7 %copy-start.32 = (f32[512,8]{0,1:T(8,128)}, f32[512,8]{0,1:T(8,128)S(1)}, u32[]{:S(2)}) copy-start(f32[512,8]{0,1:T(8,128)S(1)} %get-tuple-element.1184) | copy-start | bytes 49156
  47.5 99.7 %copy-start.34 = (f32[512,8]{0,1:T(8,128)}, f32[512,8]{0,1:T(8,128)S(1)}, u32[]{:S(2)}) copy-start(f32[512,8]{0,1:T(8,128)S(1)} %get-tuple-element.1185) | copy-start | bytes 49156
  148.2 93.0 %all-gather.19.cloned.1.call-start = ((), (), s32[]{:S(2)}) async-start(), calls=%async_computation.9 | async-start | bytes 4718592 | tf_op jit(solution)/shard_map/all_gather | solution.py:340
  150.4 190.3 %all-gather.21.cloned.1.call-start = ((), (), s32[]{:S(2)}) async-start(), calls=%async_computation.10 | async-start | bytes 2359296 | tf_op jit(solution)/shard_map/all_gather | solution.py:301
  151.2 297.1 %all-reduce.11.cloned.1.call-start = ((), (), s32[]{:S(2)}) async-start(), calls=%async_computation.11 | async-start | bytes 8388608 | tf_op jit(solution)/shard_map/psum | solution.py:350
  345.7 212.8 %all-gather.23.cloned.1.call-start = ((), (), s32[]{:S(2)}) async-start(), calls=%async_computation.12 | async-start | bytes 12976128 | tf_op jit(solution)/shard_map/all_gather | solution.py:304
  348.9 262.3 %all-gather.27.cloned.1.call-start = ((), (), s32[]{:S(2)}) async-start(), calls=%async_computation.14 | async-start | bytes 5242880 | tf_op jit(solution)/shard_map/all_gather | solution.py:309
  349.7 324.6 %all-gather.25.cloned.1.call-start = ((), (), s32[]{:S(2)}) async-start(), calls=%async_computation.13 | async-start | bytes 6488064 | tf_op jit(solution)/shard_map/all_gather | solution.py:305
  351.4 447.8 %all-reduce.13.cloned.1.call-start = ((), (), s32[]{:S(2)}) async-start(), calls=%async_computation.15 | async-start | bytes 8388608 | tf_op jit(solution)/shard_map/psum | solution.py:385
  361.1 197.5 %copy-start.60 = (f32[8,1,256]{2,1,0:T(1,128)}, f32[8,1,256]{2,1,0:T(1,128)S(1)}, u32[]{:S(2)}) copy-start(f32[8,1,256]{2,1,0:T(1,128)S(1)} %convert_element_type.273) | copy-start | bytes 24580
  370.4 434.3 %copy-start.36 = (f32[8,1,256]{2,1,0:T(1,128)}, f32[8,1,256]{2,1,0:T(1,128)S(1)}, u32[]{:S(2)}) copy-start(f32[8,1,256]{2,1,0:T(1,128)S(1)} %convert_element_type.272) | copy-start | bytes 24580
  452.3 352.4 %copy-start.44 = (f32[512]{0:T(512)}, f32[512]{0:T(512)S(1)}, u32[]{:S(2)}) copy-start(f32[512]{0:T(512)S(1)} %broadcast_multiply_fusion.5) | copy-start | bytes 6148
  454.3 350.4 %copy-start.51 = (f32[512]{0:T(512)}, f32[512]{0:T(512)S(1)}, u32[]{:S(2)}) copy-start(f32[512]{0:T(512)S(1)} %add_rsqrt_fusion) | copy-start | bytes 6148
  697.2 518.9 %reduce-scatter.8.cloned.1.call-start = ((), (), s32[]{:S(2)}) async-start(), calls=%async_computation.16 | async-start | bytes 9437184 | tf_op jit(solution)/shard_map/reduce_scatter | solution.py:422
  1115.3 191.0 %reduce-scatter.10.cloned.1.call-start = ((), (), s32[]{:S(2)}) async-start(), calls=%async_computation.17 | async-start | bytes 9437184 | tf_op jit(solution)/shard_map/reduce_scatter | solution.py:423
  1115.9 241.7 %reduce-scatter.14.cloned.1.call-start = ((), (), s32[]{:S(2)}) async-start(), calls=%async_computation.19 | async-start | bytes 4718592 | tf_op jit(solution)/shard_map/reduce_scatter | solution.py:458
  1121.9 356.1 %reduce-scatter.18.cloned.1.call-start = ((), (), s32[]{:S(2)}) async-start(), calls=%async_computation.21 | async-start | bytes 12976128 | tf_op jit(solution)/shard_map/reduce_scatter | solution.py:462
  1133.2 518.9 %all-reduce.15.cloned.1.call-start = ((), (), s32[]{:S(2)}) async-start(), calls=%async_computation.22 | async-start | bytes 16777216 | tf_op jit(solution)/shard_map/psum | solution.py:363
  1142.1 75.3 %copy-start.18 = (bf16[512,8,64]{0,2,1:T(8,128)(2,1)}, bf16[512,8,64]{0,2,1:T(8,128)(2,1)S(1)}, u32[]{:S(2)}) copy-start(bf16[512,8,64]{0,2,1:T(8,128)(2,1)S(1)} %maximum_bitcast_fusion.2) | copy-start | bytes 1572868
  1217.4 90.2 %copy-start.33 = (f32[512,8]{0,1:T(8,128)S(1)}, f32[512,8]{0,1:T(8,128)}, u32[]{:S(2)}) copy-start(f32[512,8]{0,1:T(8,128)} %copy-done.32) | copy-start | bytes 49156
  1217.6 90.8 %slice-start = ((bf16[512,8,64]{0,2,1:T(8,128)(2,1)}), bf16[512,8,48]{0,2,1:T(8,128)(2,1)S(1)}, s32[]{:S(2)}) async-start(bf16[512,8,64]{0,2,1:T(8,128)(2,1)} %copy-done.18), calls=%async_computation.23 | async-start | bytes 786432 | tf_op jit(solution)/shard_map/slice | solution.py:69
  1316.6 566.9 %reduce-scatter.16.cloned.1.call-start = ((), (), s32[]{:S(2)}) async-start(), calls=%async_computation.20 | async-start | bytes 25952256 | tf_op jit(solution)/shard_map/reduce_scatter | solution.py:461
  1330.9 683.1 %reduce-scatter.12.cloned.1.call-start = ((), (), s32[]{:S(2)}) async-start(), calls=%async_computation.18 | async-start | bytes 14155776 | tf_op jit(solution)/shard_map/reduce_scatter | solution.py:456
  1340.6 137.4 %copy-start.17 = (f32[1408,256]{1,0:T(8,128)S(1)}, f32[1408,256]{1,0:T(8,128)}, u32[]{:S(2)}) copy-start(f32[1408,256]{1,0:T(8,128)} %param.61) | copy-start | bytes 4325380
  1360.0 292.2 %copy-start.43 = (f32[512]{0:T(512)S(1)}, f32[512]{0:T(512)}, u32[]{:S(2)}) copy-start(f32[512]{0:T(512)} %copy-done.42) | copy-start | bytes 6148
  1652.2 37.3 %copy-start.63 = (f32[256]{0:T(256)S(1)}, f32[256]{0:T(256)}, u32[]{:S(2)}) copy-start(f32[256]{0:T(256)} %param.53) | copy-start | bytes 3076
  1652.2 37.3 %copy-start.64 = (f32[256]{0:T(256)S(1)}, f32[256]{0:T(256)}, u32[]{:S(2)}) copy-start(f32[256]{0:T(256)} %param.62) | copy-start | bytes 3076
  1652.2 37.3 %copy-start.65 = (f32[256]{0:T(256)S(1)}, f32[256]{0:T(256)}, u32[]{:S(2)}) copy-start(f32[256]{0:T(256)} %param.71) | copy-start | bytes 3076
  1652.2 37.9 %copy-start.67 = (f32[256]{0:T(256)S(1)}, f32[256]{0:T(256)}, u32[]{:S(2)}) copy-start(f32[256]{0:T(256)} %param.54) | copy-start | bytes 3076
  1652.2 37.9 %copy-start.68 = (f32[256]{0:T(256)S(1)}, f32[256]{0:T(256)}, u32[]{:S(2)}) copy-start(f32[256]{0:T(256)} %param.63) | copy-start | bytes 3076
  1652.2 37.9 %copy-start.69 = (f32[256]{0:T(256)S(1)}, f32[256]{0:T(256)}, u32[]{:S(2)}) copy-start(f32[256]{0:T(256)} %param.72) | copy-start | bytes 3076
  1652.3 38.6 %copy-start.71 = (f32[256]{0:T(256)S(1)}, f32[256]{0:T(256)}, u32[]{:S(2)}) copy-start(f32[256]{0:T(256)} %param.58) | copy-start | bytes 3076
  1652.3 38.6 %copy-start.72 = (f32[256]{0:T(256)S(1)}, f32[256]{0:T(256)}, u32[]{:S(2)}) copy-start(f32[256]{0:T(256)} %param.67) | copy-start | bytes 3076
  1652.3 38.6 %copy-start.73 = (f32[256]{0:T(256)S(1)}, f32[256]{0:T(256)}, u32[]{:S(2)}) copy-start(f32[256]{0:T(256)} %param.76) | copy-start | bytes 3076
  1652.3 39.2 %copy-start.75 = (f32[256]{0:T(256)S(1)}, f32[256]{0:T(256)}, u32[]{:S(2)}) copy-start(f32[256]{0:T(256)} %param.59) | copy-start | bytes 3076
  1652.3 39.2 %copy-start.76 = (f32[256]{0:T(256)S(1)}, f32[256]{0:T(256)}, u32[]{:S(2)}) copy-start(f32[256]{0:T(256)} %param.68) | copy-start | bytes 3076
  1652.3 39.2 %copy-start.77 = (f32[256]{0:T(256)S(1)}, f32[256]{0:T(256)}, u32[]{:S(2)}) copy-start(f32[256]{0:T(256)} %param.77) | copy-start | bytes 3076
  1652.3 39.9 %copy-start.39 = (f32[3,8,8]{2,1,0:T(8,128)S(1)}, f32[3,8,8]{2,1,0:T(8,128)}, u32[]{:S(2)}) copy-start(f32[3,8,8]{2,1,0:T(8,128)} %param.56) | copy-start | bytes 2308
  1652.3 39.9 %copy-start.53 = (f32[3,8,8]{2,1,0:T(8,128)S(1)}, f32[3,8,8]{2,1,0:T(8,128)}, u32[]{:S(2)}) copy-start(f32[3,8,8]{2,1,0:T(8,128)} %param.65) | copy-start | bytes 2308
  1652.3 39.8 %copy-start.54 = (f32[3,8,8]{2,1,0:T(8,128)S(1)}, f32[3,8,8]{2,1,0:T(8,128)}, u32[]{:S(2)}) copy-start(f32[3,8,8]{2,1,0:T(8,128)} %param.74) | copy-start | bytes 2308
  1900.8 113.2 %copy-start.15 = (f32[256,3,512]{2,0,1:T(8,128)S(1)}, f32[256,3,512]{2,0,1:T(8,128)}, u32[]{:S(2)}) copy-start(f32[256,3,512]{2,0,1:T(8,128)} %param.55) | copy-start | bytes 4718596
  (97 other events, 349.4 us)
Sparse Core Ops, SparseCore 0:
  9.9 55.2 all-gather.12
  67.4 65.1 all-gather.14
  148.3 45.0 all-gather.16
  195.5 45.6 all-gather.18
  243.2 29.4 all-gather.20
  345.8 102.3 all-reduce.10
  450.4 108.0 all-gather.22
  560.4 50.8 all-gather.26
  613.4 60.7 all-gather.24
  697.3 101.8 all-reduce.12
  1115.4 100.6 reduce-scatter.7
  1218.2 87.9 reduce-scatter.9
  1309.1 48.3 reduce-scatter.13
  1360.3 117.6 reduce-scatter.17
  1481.6 170.4 all-reduce.14
  1654.4 229.0 reduce-scatter.15
  1886.3 127.7 reduce-scatter.11
where the time goes:
time: 2040 us; the launch traced here: 2030 us
  waiting for transfers between devices  1300 us (64%)
  local copies, waits for them, and re-layouts  203 us (10%)
  matrix products  201 us (10%)
  other arithmetic  112 us (5%)
  loops' own time  103 us (5%)
  blocking collectives  86.2 us (4%)
    reduce_scatter x1, waiting for transfers between devices, local(): lax.psum_scatter(grad_gateup, 'ctx', scatter_dimension=0, tiled=True)  185 us
    psum x1, waiting for transfers between devices, local(): lax.psum(jnp.dot(hidden, group_down, preferred_element_type=jnp.float32),...  169 us
    reduce_scatter x1, waiting for transfers between devices, local(): lax.psum_scatter(grad_down, 'ctx', scatter_dimension=1, tiled=True)  118 us
    reduce_scatter x1, waiting for transfers between devices, local(): lax.psum_scatter(grad_project, 'ctx', scatter_dimension=0, tiled=True)  109 us
    all_gather x1, waiting for transfers between devices, local(): lax.all_gather(weight_gateup.astype(jnp.bfloat16), 'ctx', axis=0, tiled=T...  104 us
    psum x1, waiting for transfers between devices, local(): lax.psum(jnp.einsum('tgu,dgu->td', d_gate_up, back_gateup, preferred_elem...  101 us
    reduce_scatter x1, waiting for transfers between devices, local(): lax.psum_scatter(value_grads, 'ctx', scatter_dimension=0, tiled=True)  88.7 us
    psum x1, waiting for transfers between devices, local(): lax.psum(jnp.dot(mixed_heads, group_output, preferred_element_type=jnp.fl...  77.9 us
  transfers between devices with their start and end apart: 17, of which 16 were waited for; matrix products, arithmetic and copies ran while one was open for 10% of the time, Pallas kernels for 0%

commit v1 on v0

--- a/solution.py
+++ b/solution.py
@@ -4,6 +4,8 @@
 import jax
 import jax.numpy as jnp
 from jax import lax
+from jax.experimental import pallas as pl
+from jax.experimental.pallas import tpu as pltpu
 from jax.sharding import PartitionSpec as P
 
 D = 2048
@@ -33,47 +35,6 @@
     scaled = grad_out * gain_vector
     inner_mean = jnp.mean(scaled * normed, axis=-1, keepdims=True)
     return (scaled - jnp.mean(scaled, axis=-1, keepdims=True) - normed * inner_mean) * inverse
-
-
-def rotary_tables(where_at):
-    half_dims = ROT // 2
-    frequency = rope_base ** (-(jnp.arange(half_dims, dtype=jnp.float32) * 2.0) / ROT)
-    angles = where_at.astype(jnp.float32)[:, None] * frequency[None, :]
-    return (jnp.cos(angles)[:, None, :], jnp.sin(angles)[:, None, :])
-
-
-def rotate(head_values, where_at):
-    cosine, sine_part = rotary_tables(where_at)
-    half_dims = ROT // 2
-    first_half = head_values[..., :half_dims]
-    second = head_values[..., half_dims:ROT]
-    return jnp.concatenate(
-        [
-            first_half * cosine - second * sine_part,
-            second * cosine + first_half * sine_part,
-            head_values[..., ROT:],
-        ],
-        axis=-1,
-    )
-
-
-def unrotate(head_grads, where_at):
-    cosine, sine_part = rotary_tables(where_at)
-    half_dims = ROT // 2
-    first_half = head_grads[..., :half_dims]
-    second = head_grads[..., half_dims:ROT]
-    return jnp.concatenate(
-        [
-            first_half * cosine + second * sine_part,
-            second * cosine - first_half * sine_part,
-            head_grads[..., ROT:],
-        ],
-        axis=-1,
-    )
-
-
-def rounded_float(values):
-    return lax.optimization_barrier(values.astype(jnp.bfloat16)).astype(jnp.float32)
 
 
 def keep_state(state_now):
@@ -240,6 +201,302 @@
     )
 
 
+F32=jnp.float32; BF=jnp.bfloat16
+score_scale = HD ** (-0.5)
+log2e = math.log2(math.e)
+neg_big = -1e30
+
+def dotf(a,b,ca,cb):
+    return lax.dot_general(a,b,(((ca,),(cb,)),((),())),preferred_element_type=F32)
+
+def place(blk_ref, r, BLK):
+    b = blk_ref[r]
+    return lax.div(b,2), pl.multiple_of(lax.rem(b,2)*BLK, BLK)
+
+def causal_mask(S):
+    return lax.broadcasted_iota(jnp.int32,(S,S),0) <= lax.broadcasted_iota(jnp.int32,(S,S),1)
+
+def fwd_kernel(blk_ref, qkv_ref, mixed_ref, full_ref, lse_ref, q_s, k_s, v_s, o_s):
+    nb, _, BLK = qkv_ref.shape
+    ns = nb//2; S = 2*BLK
+    def load(r, c):
+        u, off = place(blk_ref, r, BLK)
+        q_s[u, :, pl.ds(off,BLK)] = qkv_ref[r, 0:HD, :]
+        v_s[u, :, pl.ds(off,BLK)] = qkv_ref[r, 2*HD:3*HD, :]
+        k_s[u, pl.ds(off,BLK), :] = qkv_ref[r, HD:2*HD, :].astype(F32).T.astype(BF)
+        return c
+    lax.fori_loop(0, nb, load, 0)
+    mult = score_scale*log2e
+    def qstep(t, c):
+        qT = q_s[t]
+        def kv(u, carry, diag):
+            m, l, acc = carry
+            s = dotf(k_s[u], qT, 1, 0)
+            if diag:
+                s = jnp.where(causal_mask(S), s, neg_big)
+            m_new = jnp.maximum(m, jnp.max(s, axis=0, keepdims=True))
+            p = jnp.exp2(s*mult - m_new*mult)
+            alpha = jnp.exp2((m-m_new)*mult)
+            l = l*alpha + jnp.sum(p, axis=0, keepdims=True)
+            acc = acc*alpha + dotf(v_s[u], p.astype(BF), 1, 0)
+            return m_new, l, acc
+        init = (jnp.full((1,S),neg_big,F32), jnp.zeros((1,S),F32), jnp.zeros((HD,S),F32))
+        carry = lax.fori_loop(0, t, lambda u,cc: kv(u,cc,False), init)
+        m, l, acc = kv(t, carry, True)
+        o_s[t] = acc / l
+        lse_ref[t] = m*mult + jnp.log2(l)
+        return c
+    lax.fori_loop(0, ns, qstep, 0)
+    def put(r, c):
+        u, off = place(blk_ref, r, BLK)
+        o = o_s[u, :, pl.ds(off,BLK)]
+        full_ref[r] = o
+        mixed_ref[r] = o.astype(BF)
+        return c
+    lax.fori_loop(0, nb, put, 0)
+
+def bwd_kernel(blk_ref, qkv_ref, do_ref, full_ref, lse_ref, dqkv_ref, q_s, k_s, v_s, g_s, kT_s, qn_s, gn_s, dq_s, dk_s, dv_s, dl_s):
+    nb, _, BLK = qkv_ref.shape
+    ns = nb//2; S = 2*BLK
+    def load(r, c):
+        u, off = place(blk_ref, r, BLK)
+        q = qkv_ref[r, 0:HD, :]; k = qkv_ref[r, HD:2*HD, :]; v = qkv_ref[r, 2*HD:3*HD, :]; g = do_ref[r]
+        q_s[u, :, pl.ds(off,BLK)] = q
+        g_s[u, :, pl.ds(off,BLK)] = g
+        kT_s[u, :, pl.ds(off,BLK)] = k
+        k_s[u, pl.ds(off,BLK), :] = k.astype(F32).T.astype(BF)
+        v_s[u, pl.ds(off,BLK), :] = v.astype(F32).T.astype(BF)
+        qn_s[u, pl.ds(off,BLK), :] = q.astype(F32).T.astype(BF)
+        gn_s[u, pl.ds(off,BLK), :] = g.astype(F32).T.astype(BF)
+        dl_s[u, :, pl.ds(off,BLK)] = jnp.sum(g.astype(F32)*full_ref[r], axis=0, keepdims=True)
+        return c
+    lax.fori_loop(0, nb, load, 0)
+    mult = score_scale*log2e
+    def kvstep(i, c):
+        u = ns-1-i
+        k = k_s[u]; v = v_s[u]; kT = kT_s[u]
+        def pair(t, diag):
+            s = dotf(k, q_s[t], 1, 0)
+            if diag:
+                s = jnp.where(causal_mask(S), s, neg_big)
+            p = jnp.exp2(s*mult - lse_ref[t])
+            dp = dotf(v, g_s[t], 1, 0)
+            ds = (p*(dp - dl_s[t])).astype(BF)
+            dv = dotf(p.astype(BF), gn_s[t], 1, 0)
+            dk = dotf(ds, qn_s[t], 1, 0)
+            dq = dotf(kT, ds, 1, 0)
+            return dq, dk, dv
+        dq, dk, dv = pair(u, True)
+        dq_s[u] = dq
+        def step(t, carry):
+            dk, dv = carry
+            a, b, e = pair(t, False)
+            dq_s[t] += a
+            return dk+b, dv+e
+        dk, dv = lax.fori_loop(u+1, ns, step, (dk, dv))
+        dk_s[u] = dk; dv_s[u] = dv
+        return c
+    lax.fori_loop(0, ns, kvstep, 0)
+    def put(r, c):
+        u, off = place(blk_ref, r, BLK)
+        dqkv_ref[r, 0:HD, :] = (dq_s[u, :, pl.ds(off,BLK)]*score_scale).astype(BF)
+        dqkv_ref[r, HD:2*HD, :] = (dk_s[u, pl.ds(off,BLK), :]*score_scale).T.astype(BF)
+        dqkv_ref[r, 2*HD:3*HD, :] = dv_s[u, pl.ds(off,BLK), :].T.astype(BF)
+        return c
+    lax.fori_loop(0, nb, put, 0)
+
+VM = lambda: pl.BlockSpec(memory_space=pltpu.VMEM)
+SM = lambda: pl.BlockSpec(memory_space=pltpu.SMEM)
+
+def attend(blk, qkv):
+    nb,_,BLK = qkv.shape; ns=nb//2; S=2*BLK
+    sds=jax.ShapeDtypeStruct
+    pairs = ns*(ns+1)//2
+    return pl.pallas_call(fwd_kernel,
+        out_shape=(sds((nb,HD,BLK),BF), sds((nb,HD,BLK),F32), sds((ns,1,S),F32)),
+        in_specs=[SM(), VM()], out_specs=(VM(),VM(),VM()),
+        scratch_shapes=[pltpu.VMEM((ns,HD,S),BF), pltpu.VMEM((ns,S,HD),BF), pltpu.VMEM((ns,HD,S),BF), pltpu.VMEM((ns,HD,S),F32)],
+        compiler_params=pltpu.CompilerParams(vmem_limit_bytes=48*2**20),
+        cost_estimate=pl.CostEstimate(flops=pairs*S*S*HD*4, bytes_accessed=nb*BLK*HD*12, transcendentals=pairs*S*S),
+        name="attend_forward")(blk, qkv)
+
+def attend_back(blk, qkv, do, full, lse):
+    nb,_,BLK = qkv.shape; ns=nb//2; S=2*BLK
+    pairs = ns*(ns+1)//2
+    V=lambda s,d: pltpu.VMEM(s,d)
+    return pl.pallas_call(bwd_kernel,
+        out_shape=jax.ShapeDtypeStruct((nb,3*HD,BLK),BF),
+        in_specs=[SM(), VM(), VM(), VM(), VM()], out_specs=VM(),
+        scratch_shapes=[V((ns,HD,S),BF), V((ns,S,HD),BF), V((ns,S,HD),BF), V((ns,HD,S),BF), V((ns,HD,S),BF), V((ns,S,HD),BF), V((ns,S,HD),BF),
+          V((ns,HD,S),F32), V((ns,S,HD),F32), V((ns,S,HD),F32), V((ns,1,S),F32)],
+        compiler_params=pltpu.CompilerParams(vmem_limit_bytes=56*2**20),
+        cost_estimate=pl.CostEstimate(flops=pairs*S*S*HD*10, bytes_accessed=nb*BLK*HD*18, transcendentals=pairs*S*S),
+        name="attend_backward")(blk, qkv, do, full, lse)
+
+
+def rotary_rows(where_at):
+    half_dims = ROT // 2
+    frequency = rope_base ** (-(jnp.arange(half_dims, dtype=jnp.float32) * 2.0) / ROT)
+    angles = frequency[:, None] * where_at.astype(jnp.float32)[None, :]
+    return (jnp.cos(angles), jnp.sin(angles))
+
+
+def turn(columns, cosine, sine_part):
+    half_dims = ROT // 2
+    first_half = columns[:, :half_dims]
+    second = columns[:, half_dims:ROT]
+    return jnp.concatenate(
+        [
+            first_half * cosine - second * sine_part,
+            second * cosine + first_half * sine_part,
+            columns[:, ROT:],
+        ],
+        axis=1,
+    )
+
+
+def exchange(values):
+    return lax.all_to_all(values, "ctx", split_axis=0, concat_axis=0, tiled=True)
+
+
+def blocks_out(columns, blocks):
+    parts, heads, _, rows = columns.shape
+    split = columns.reshape(parts, heads, HD, blocks, rows // blocks)
+    return jnp.transpose(split, (1, 3, 0, 2, 4)).reshape(heads, blocks, parts * HD, rows // blocks)
+
+
+def blocks_in(arrived, parts):
+    heads, blocks, _, block_rows = arrived.shape
+    split = arrived.reshape(heads, blocks, parts, HD, block_rows)
+    return jnp.transpose(split, (2, 0, 3, 1, 4)).reshape(parts, heads, HD, blocks * block_rows)
+
+
+def by_head_forward(turned, positions, contexts):
+    rows = turned.shape[-1]
+    block_rows = rows // 2
+    block_ids = positions[::block_rows] // block_rows
+    arrived = exchange(blocks_out(turned, 2)).reshape(2 * contexts, 3 * HD, block_rows)
+    mixed, full, lse = attend(block_ids, arrived)
+    back = exchange(mixed.reshape(contexts, 2, HD, block_rows))
+    mixed_columns = blocks_in(back, 1).reshape(-1, rows)
+    return mixed_columns, (block_ids, arrived, full, lse)
+
+
+def by_head_backward(d_mixed, kept):
+    block_ids, arrived, full, lse = kept
+    heads = d_mixed.shape[0] // HD
+    rows = d_mixed.shape[1]
+    sent = exchange(blocks_out(d_mixed.reshape(1, heads, HD, rows), 2))
+    grads = attend_back(block_ids, arrived, sent.reshape(full.shape), full, lse)
+    back = exchange(grads.reshape(heads, 2, 3 * HD, rows // 2))
+    return blocks_in(back, 3)
+
+
+def by_rows_forward(turned, positions, row_pos):
+    heads_here, rows = turned.shape[1], turned.shape[3]
+    half_rows = rows // 2
+    rows_first = jnp.transpose(turned, (0, 3, 1, 2))
+    query_heads = rows_first[0]
+    head_key = rows_first[1].reshape(rows, heads_here * HD)
+    head_value = rows_first[2].reshape(rows, heads_here * HD)
+    pos_halves = (row_pos[:half_rows], row_pos[half_rows:])
+    query_halves = (query_heads[:half_rows], query_heads[half_rows:])
+    start_state = (
+        jnp.full((heads_here, half_rows), masked_score, jnp.float32),
+        jnp.zeros((heads_here, half_rows), jnp.float32),
+        jnp.zeros((heads_here, half_rows, HD), jnp.float32),
+    )
+    attend_fns = (
+        partial(attend_block, query_halves[0], pos_halves[0]),
+        partial(attend_block, query_halves[1], pos_halves[1]),
+    )
+    states = query_side_fold(
+        attend_fns,
+        pos_halves,
+        positions,
+        rows,
+        (start_state, start_state),
+        (
+            lax.all_gather(head_key, "ctx", axis=0, tiled=True),
+            lax.all_gather(head_value, "ctx", axis=0, tiled=True),
+        ),
+    )
+    lse_halves = (states[0][0] + jnp.log(states[0][1]), states[1][0] + jnp.log(states[1][1]))
+    attended = jnp.concatenate(
+        [states[0][2] / states[0][1][..., None], states[1][2] / states[1][1][..., None]], axis=1
+    )
+    mixed_columns = jnp.transpose(attended, (0, 2, 1)).reshape(heads_here * HD, rows)
+    kept = (query_halves, pos_halves, head_key, head_value, lse_halves, attended)
+    return mixed_columns.astype(jnp.bfloat16), kept
+
+
+def by_rows_backward(d_mixed, positions, kept, contexts):
+    query_halves, pos_halves, head_key, head_value, lse_halves, attended = kept
+    heads_here, rows, _ = attended.shape
+    half_rows = rows // 2
+    grad_heads = jnp.transpose(d_mixed.reshape(heads_here, HD, rows), (2, 0, 1))
+    row_delta = jnp.sum(
+        jnp.transpose(grad_heads.astype(jnp.float32), (1, 0, 2)) * attended, axis=-1
+    )
+    grad_halves = (grad_heads[:half_rows], grad_heads[half_rows:])
+    delta_halves = (row_delta[:, :half_rows], row_delta[:, half_rows:])
+    zero_query = jnp.zeros((heads_here, half_rows, HD), jnp.float32)
+    zero_keys = jnp.zeros((rows * contexts, heads_here * HD), jnp.float32)
+    query_grads, key_grads, value_grads = backward_fold(
+        query_halves,
+        pos_halves,
+        grad_halves,
+        lse_halves,
+        delta_halves,
+        positions,
+        rows,
+        ((zero_query, zero_query), zero_keys, zero_keys),
+        (
+            lax.all_gather(head_key, "ctx", axis=0, tiled=True),
+            lax.all_gather(head_value, "ctx", axis=0, tiled=True),
+        ),
+    )
+    query_columns = jnp.transpose(jnp.concatenate(query_grads, axis=1), (0, 2, 1))
+
+    def own_columns(grads):
+        own = lax.psum_scatter(grads, "ctx", scatter_dimension=0, tiled=True)
+        return jnp.transpose(own.reshape(rows, heads_here, HD), (1, 2, 0))
+
+    columns = jnp.stack([query_columns, own_columns(key_grads), own_columns(value_grads)])
+    return columns.astype(jnp.bfloat16)
+
+
+def gather_tokens(values):
+    return lax.all_gather(values, "fsdp", axis=0, tiled=True)
+
+
+def scatter_tokens(partial_rows):
+    summed = lax.psum_scatter(
+        partial_rows.astype(jnp.bfloat16), "fsdp", scatter_dimension=0, tiled=True
+    )
+    return summed.astype(jnp.float32)
+
+
+def scatter_grad(grad_value, dimension):
+    summed = lax.psum_scatter(
+        grad_value.astype(jnp.bfloat16), "ctx", scatter_dimension=dimension, tiled=True
+    )
+    return summed.astype(jnp.float32)
+
+
+def gather_small(gain_one, shift_one, gain_two, shift_two, bias):
+    width = gain_one.shape[0]
+    packed = jnp.concatenate([gain_one, shift_one, gain_two, shift_two, bias.reshape(-1)])
+    whole = lax.all_gather(packed.astype(jnp.bfloat16), "ctx", axis=0, tiled=False)
+    vectors = [
+        whole[:, index * width : (index + 1) * width].reshape(-1).astype(jnp.float32)
+        for index in range(4)
+    ]
+    parts = whole[:, 4 * width :].reshape((-1,) + bias.shape)
+    columns = jnp.transpose(parts, (1, 2, 0, 3)).reshape(3, bias.shape[1], HD)
+    return vectors + [columns.astype(jnp.float32)]
+
+
 def local(
     inputs,
     cotangent,
@@ -276,192 +533,112 @@
     groups = lax.axis_size("fsdp")
     contexts = lax.axis_size("ctx")
     heads_here = H // groups
-    width_here = heads_here * HD
     row_count = tokens * groups
-    half_rows = row_count // 2
-    total_keys = row_count * contexts
+    spread_heads = heads_here == contexts
     row_pos = lax.dynamic_slice_in_dim(positions, lax.axis_index("ctx") * row_count, row_count)
-    own_start = lax.axis_index("fsdp") * tokens
-    pos_halves = (row_pos[:half_rows], row_pos[half_rows:])
-    (
-        gain_one,
-        shift_one,
-        group_project,
-        group_bias,
-        group_output,
-        gain_two,
-        shift_two,
-        group_gateup,
-        group_down,
-    ) = (
-        lax.all_gather(gain_attention.astype(jnp.bfloat16), "ctx", axis=0, tiled=True),
-        lax.all_gather(shift_attention.astype(jnp.bfloat16), "ctx", axis=0, tiled=True),
-        lax.all_gather(weight_project.astype(jnp.bfloat16), "ctx", axis=0, tiled=True),
-        lax.all_gather(bias_project.astype(jnp.bfloat16), "ctx", axis=2, tiled=True),
-        lax.all_gather(weight_output.astype(jnp.bfloat16), "ctx", axis=1, tiled=True),
-        lax.all_gather(gain_feedforward.astype(jnp.bfloat16), "ctx", axis=0, tiled=True),
-        lax.all_gather(shift_feedforward.astype(jnp.bfloat16), "ctx", axis=0, tiled=True),
-        lax.all_gather(weight_gateup.astype(jnp.bfloat16), "ctx", axis=0, tiled=True),
-        lax.all_gather(weight_down.astype(jnp.bfloat16), "ctx", axis=1, tiled=True),
-    )
-    group_inputs, group_cotangent = (
-        lax.all_gather(inputs, "fsdp", axis=0, tiled=True),
-        lax.all_gather(cotangent, "fsdp", axis=0, tiled=True),
-    )
-    normed_one, inverse_one = norm_parts(group_inputs)
-    first_act = (normed_one * gain_one.astype(jnp.float32) + shift_one.astype(jnp.float32)).astype(
-        jnp.bfloat16
-    )
-    projected = jnp.dot(
-        first_act, group_project.reshape(D, 3 * width_here), preferred_element_type=jnp.float32
-    ) + group_bias.reshape(3 * width_here).astype(jnp.float32)
-    split_cols = projected.reshape(row_count, 3, heads_here, HD)
-    query_heads = rotate(split_cols[:, 0], row_pos).astype(jnp.bfloat16)
-    head_key = rotate(split_cols[:, 1], row_pos).reshape(row_count, width_here).astype(jnp.bfloat16)
-    head_value = split_cols[:, 2].reshape(row_count, width_here).astype(jnp.bfloat16)
-    query_halves = (query_heads[:half_rows], query_heads[half_rows:])
-    start_state = (
-        jnp.full((heads_here, half_rows), masked_score, jnp.float32),
-        jnp.zeros((heads_here, half_rows), jnp.float32),
-        jnp.zeros((heads_here, half_rows, HD), jnp.float32),
-    )
-    attend_fns = (
-        partial(attend_block, query_halves[0], pos_halves[0]),
-        partial(attend_block, query_halves[1], pos_halves[1]),
-    )
-    states = query_side_fold(
-        attend_fns,
-        pos_halves,
-        positions,
-        row_count,
-        (start_state, start_state),
-        (
-            lax.all_gather(head_key, "ctx", axis=0, tiled=True),
-            lax.all_gather(head_value, "ctx", axis=0, tiled=True),
-        ),
-    )
-    lse_halves = (states[0][0] + jnp.log(states[0][1]), states[1][0] + jnp.log(states[1][1]))
-    attended = jnp.concatenate(
-        [states[0][2] / states[0][1][..., None], states[1][2] / states[1][1][..., None]], axis=1
-    )
-    mixed_heads = (
-        jnp.transpose(attended, (1, 0, 2)).reshape(row_count, width_here).astype(jnp.bfloat16)
-    )
-    middle = group_inputs + lax.psum(
-        jnp.dot(mixed_heads, group_output, preferred_element_type=jnp.float32), "fsdp"
+    cosine, sine_part = rotary_rows(row_pos)
+    gain_one, shift_one, gain_two, shift_two, group_bias = gather_small(
+        gain_attention, shift_attention, gain_feedforward, shift_feedforward, bias_project
+    )
+    group_project = lax.all_gather(weight_project.astype(jnp.bfloat16), "ctx", axis=0, tiled=True)
+    group_output = lax.all_gather(weight_output.astype(jnp.bfloat16), "ctx", axis=1, tiled=True)
+    group_gateup = lax.all_gather(weight_gateup.astype(jnp.bfloat16), "ctx", axis=0, tiled=True)
+    group_down = lax.all_gather(weight_down.astype(jnp.bfloat16), "ctx", axis=1, tiled=True)
+    normed_one, inverse_one = norm_parts(inputs)
+    first_act = gather_tokens((normed_one * gain_one + shift_one).astype(jnp.bfloat16))
+    d_branch = gather_tokens(cotangent.astype(jnp.bfloat16))
+    projected = (
+        jnp.einsum("dge,td->get", group_project, first_act, preferred_element_type=jnp.float32)
+        .reshape(3, heads_here, HD, row_count)
+        + group_bias[..., None]
+    )
+    turned = jnp.stack(
+        [
+            turn(projected[0], cosine, sine_part),
+            turn(projected[1], cosine, sine_part),
+            projected[2],
+        ]
+    ).astype(jnp.bfloat16)
+    if spread_heads:
+        mixed, kept = by_head_forward(turned, positions, contexts)
+    else:
+        mixed, kept = by_rows_forward(turned, positions, row_pos)
+    middle = inputs + scatter_tokens(
+        jnp.einsum("et,ed->td", mixed, group_output, preferred_element_type=jnp.float32)
     )
     normed_two, inverse_two = norm_parts(middle)
-    second_act = (normed_two * gain_two.astype(jnp.float32) + shift_two.astype(jnp.float32)).astype(
-        jnp.bfloat16
-    )
-    gate_up = jnp.einsum(
-        "td,dgu->tgu", second_act, group_gateup, preferred_element_type=jnp.float32
-    )
-    gate_part = gate_up[:, 0]
-    up_part = gate_up[:, 1]
+    second_act = gather_tokens((normed_two * gain_two + shift_two).astype(jnp.bfloat16))
+    gate_part = jnp.dot(second_act, group_gateup[:, 0], preferred_element_type=jnp.float32)
+    up_part = jnp.dot(second_act, group_gateup[:, 1], preferred_element_type=jnp.float32)
     hidden = (jax.nn.silu(gate_part) * up_part).astype(jnp.bfloat16)
-    output_rows = middle + lax.psum(
-        jnp.dot(hidden, group_down, preferred_element_type=jnp.float32), "fsdp"
-    )
-    output = lax.dynamic_slice_in_dim(output_rows, own_start, tokens)
-    back_gain_one, back_project, back_output, back_gain_two, back_gateup, back_down = (
-        lax.all_gather(gain_attention.astype(jnp.bfloat16), "ctx", axis=0, tiled=True),
-        lax.all_gather(weight_project.astype(jnp.bfloat16), "ctx", axis=0, tiled=True),
-        lax.all_gather(weight_output.astype(jnp.bfloat16), "ctx", axis=1, tiled=True),
-        lax.all_gather(gain_feedforward.astype(jnp.bfloat16), "ctx", axis=0, tiled=True),
-        lax.all_gather(weight_gateup.astype(jnp.bfloat16), "ctx", axis=0, tiled=True),
-        lax.all_gather(weight_down.astype(jnp.bfloat16), "ctx", axis=1, tiled=True),
-    )
-    d_branch = group_cotangent.astype(jnp.bfloat16)
+    output = middle + scatter_tokens(
+        jnp.dot(hidden, group_down, preferred_element_type=jnp.float32)
+    )
     grad_down = jnp.einsum("tu,td->ud", hidden, d_branch, preferred_element_type=jnp.float32)
-    d_hidden = jnp.einsum("td,ud->tu", d_branch, back_down, preferred_element_type=jnp.float32)
+    d_hidden = jnp.einsum("td,ud->tu", d_branch, group_down, preferred_element_type=jnp.float32)
     gate_sigmoid = jax.nn.sigmoid(gate_part)
     d_gate = d_hidden * up_part * gate_sigmoid * (1.0 + gate_part * (1.0 - gate_sigmoid))
     d_up = d_hidden * jax.nn.silu(gate_part)
-    d_gate_up = jnp.stack([d_gate, d_up], axis=1).astype(jnp.bfloat16)
+    d_gate_up = jnp.stack([d_gate, d_up], axis=0).astype(jnp.bfloat16)
     grad_gateup = jnp.einsum(
-        "td,tgu->dgu", second_act, d_gate_up, preferred_element_type=jnp.float32
-    )
-    d_second = lax.psum(
-        jnp.einsum("tgu,dgu->td", d_gate_up, back_gateup, preferred_element_type=jnp.float32),
-        "fsdp",
-    )
-    grad_gain_two = jnp.sum(d_second * normed_two, axis=0)
-    grad_shift_two = jnp.sum(d_second, axis=0)
-    d_middle = group_cotangent + norm_back(
-        d_second, normed_two, inverse_two, back_gain_two.astype(jnp.float32)
-    )
-    d_attend = d_middle.astype(jnp.bfloat16)
-    grad_output = jnp.einsum("te,td->ed", mixed_heads, d_attend, preferred_element_type=jnp.float32)
+        "td,gtu->dgu", second_act, d_gate_up, preferred_element_type=jnp.float32
+    )
+    d_second = scatter_tokens(
+        jnp.einsum("gtu,dgu->td", d_gate_up, group_gateup, preferred_element_type=jnp.float32)
+    )
+    d_middle = cotangent + norm_back(d_second, normed_two, inverse_two, gain_two)
+    d_attend = gather_tokens(d_middle.astype(jnp.bfloat16))
+    grad_output = jnp.einsum("et,td->ed", mixed, d_attend, preferred_element_type=jnp.float32)
     d_mixed = jnp.einsum(
-        "td,ed->te", d_attend, back_output, preferred_element_type=jnp.float32
+        "ed,td->et", group_output, d_attend, preferred_element_type=jnp.float32
     ).astype(jnp.bfloat16)
-    grad_heads = d_mixed.reshape(row_count, heads_here, HD)
-    row_delta = jnp.sum(
-        jnp.transpose(grad_heads.astype(jnp.float32), (1, 0, 2)) * attended, axis=-1
-    )
-    grad_halves = (grad_heads[:half_rows], grad_heads[half_rows:])
-    delta_halves = (row_delta[:, :half_rows], row_delta[:, half_rows:])
-    zero_query = jnp.zeros((heads_here, half_rows, HD), jnp.float32)
-    zero_keys = jnp.zeros((total_keys, width_here), jnp.float32)
-    query_grads, key_grads, value_grads = backward_fold(
-        query_halves,
-        pos_halves,
-        grad_halves,
-        lse_halves,
-        delta_halves,
-        positions,
-        row_count,
-        ((zero_query, zero_query), zero_keys, zero_keys),
-        (
-            lax.all_gather(head_key, "ctx", axis=0, tiled=True),
-            lax.all_gather(head_value, "ctx", axis=0, tiled=True),
+    if spread_heads:
+        columns = by_head_backward(d_mixed, kept)
+    else:
+        columns = by_rows_backward(d_mixed, positions, kept, contexts)
+    columns = columns.astype(jnp.float32)
+    d_projected = jnp.stack(
+        [
+            turn(columns[0], cosine, -sine_part),
+            turn(columns[1], cosine, -sine_part),
+            columns[2],
+        ]
+    ).astype(jnp.bfloat16)
+    grad_bias = jnp.sum(d_projected.astype(jnp.float32), axis=-1)
+    d_flat = d_projected.reshape(3, heads_here * HD, row_count)
+    grad_project = jnp.einsum(
+        "td,get->dge", first_act, d_flat, preferred_element_type=jnp.float32
+    )
+    d_first = scatter_tokens(
+        jnp.einsum("get,dge->td", d_flat, group_project, preferred_element_type=jnp.float32)
+    )
+    input_grad = d_middle + norm_back(d_first, normed_one, inverse_one, gain_one)
+    vector_grads = lax.psum(
+        jnp.stack(
+            [
+                jnp.sum(d_first * normed_one, axis=0),
+                jnp.sum(d_first, axis=0),
+                jnp.sum(d_second * normed_two, axis=0),
+                jnp.sum(d_second, axis=0),
+            ]
         ),
-    )
-    summed_keys, summed_values = (
-        lax.psum_scatter(key_grads, "ctx", scatter_dimension=0, tiled=True),
-        lax.psum_scatter(value_grads, "ctx", scatter_dimension=0, tiled=True),
-    )
-    query_rows = jnp.transpose(jnp.concatenate([query_grads[0], query_grads[1]], axis=1), (1, 0, 2))
-    query_back = unrotate(rounded_float(query_rows), row_pos)
-    key_back = unrotate(rounded_float(summed_keys.reshape(row_count, heads_here, HD)), row_pos)
-    value_back = (
-        summed_values.reshape(row_count, heads_here, HD).astype(jnp.bfloat16).astype(jnp.float32)
-    )
-    d_projected = jnp.stack([query_back, key_back, value_back], axis=1).astype(jnp.bfloat16)
-    grad_bias = jnp.sum(d_projected.astype(jnp.float32), axis=0)
-    d_flat = d_projected.reshape(row_count, 3 * width_here)
-    grad_project = jnp.einsum(
-        "td,te->de", first_act, d_flat, preferred_element_type=jnp.float32
-    ).reshape(D, 3, width_here)
-    d_first = lax.psum(
-        jnp.einsum(
-            "te,de->td",
-            d_flat,
-            back_project.reshape(D, 3 * width_here),
-            preferred_element_type=jnp.float32,
-        ),
-        "fsdp",
-    )
-    grad_gain_one = jnp.sum(d_first * normed_one, axis=0)
-    grad_shift_one = jnp.sum(d_first, axis=0)
-    input_rows = d_middle + norm_back(
-        d_first, normed_one, inverse_one, back_gain_one.astype(jnp.float32)
-    )
-    input_grad = lax.dynamic_slice_in_dim(input_rows, own_start, tokens)
-    gradients = list(
-        (
-            lax.psum_scatter(grad_gain_one, "ctx", scatter_dimension=0, tiled=True),
-            lax.psum_scatter(grad_shift_one, "ctx", scatter_dimension=0, tiled=True),
-            lax.psum_scatter(grad_project, "ctx", scatter_dimension=0, tiled=True),
-            lax.psum_scatter(grad_bias, "ctx", scatter_dimension=2, tiled=True),
-            lax.psum_scatter(grad_output, "ctx", scatter_dimension=1, tiled=True),
-            lax.psum_scatter(grad_gain_two, "ctx", scatter_dimension=0, tiled=True),
-            lax.psum_scatter(grad_shift_two, "ctx", scatter_dimension=0, tiled=True),
-            lax.psum_scatter(grad_gateup, "ctx", scatter_dimension=0, tiled=True),
-            lax.psum_scatter(grad_down, "ctx", scatter_dimension=1, tiled=True),
-        )
-    )
+        ("ctx", "fsdp"),
+    )
+    width = gain_attention.shape[0]
+    own_vectors = lax.dynamic_slice_in_dim(
+        vector_grads, lax.axis_index("ctx") * width, width, axis=1
+    )
+    gradients = [
+        own_vectors[0],
+        own_vectors[1],
+        scatter_grad(grad_project, 0),
+        lax.psum_scatter(grad_bias, "ctx", scatter_dimension=2, tiled=True),
+        scatter_grad(grad_output, 1),
+        own_vectors[2],
+        own_vectors[3],
+        scatter_grad(grad_gateup, 0),
+        scatter_grad(grad_down, 1),
+    ]
     params = [
         gain_attention,
         shift_attention,

time: 2040 us -> 1100 us (0.54)
  waiting for transfers between devices: 1300 us -> 605 us
  local copies, waits for them, and re-layouts: 203 us -> 63.1 us
  matrix products: 201 us -> 95 us
  blocking collectives: 86.2 us -> 190 us
  loops' own time: 103 us -> 0 us
  Pallas kernels: 0 us -> 62.3 us
  other arithmetic: 112 us -> 56.5 us
    reduce_scatter x6 -> x8, waiting for transfers between devices: 589 us -> 189 us  [the longest x4 98.6 us: scatter_grad(): lax.psum_scatter(grad_value.astype(jnp.bfloat16), 'ctx', scatter_dimensio...]
    psum x3 -> x0, waiting for transfers between devices: 348 us -> none  [the longest x1 169 us: local(): lax.psum(jnp.dot(hidden, group_down, preferred_element_type=jnp.float32),...]
    all_to_all x0 -> x3, blocking collectives: none -> 108 us  [exchange(): lax.all_to_all(values, 'ctx', split_axis=0, concat_axis=0, tiled=True)]
    dot_general x129 -> x11, matrix products: 183 us -> 79.5 us  [the longest x1 11.1 us: local(): jnp.einsum('td,gtu->dgu', second_act, d_gate_up, preferred_element_type=j...]
    another operation x66 -> x0, loops' own time: 103 us -> none  [the longest x1 57.5 us: backward_fold(): lax.scan(backward_scan_step, states, (key_blocks, value_blocks, key_pos,...]
    dynamic_update_slice x16 -> x0, local copies, waits for them, and re-layouts: 96.3 us -> none  [the longest x8 48.2 us: backward_scan_step(): lax.dynamic_update_slice_in_dim(key_grads, jnp.concatenate(key_parts, axi...]
    pallas_call x0 -> x2, Pallas kernels: none -> 62.3 us  [the longest x1 35.4 us: attend_back(): pl.pallas_call(bwd_kernel, out_shape=jax.ShapeDtypeStruct((nb, 3 * HD, BL...]
    all_to_all x0 -> x1, waiting for transfers between devices: none -> 52.9 us  [exchange(): lax.all_to_all(values, 'ctx', split_axis=0, concat_axis=0, tiled=True)]
  transfers between devices with their start and end apart: 17 -> 17, of which waited for: 16 -> 13; matrix products, arithmetic and copies ran while one was open for 10% -> 14% of each run, Pallas kernels for 0% -> 6%
where the time goes in v1:
time: 1100 us; the launch traced here: 1090 us
  waiting for transfers between devices  605 us (55%)
  blocking collectives  190 us (17%)
  matrix products  95 us (9%)
  local copies, waits for them, and re-layouts  63.1 us (6%)
  Pallas kernels  62.3 us (6%)
  other arithmetic  56.5 us (5%)
  between operations  15.9 us (1%)
    all_gather x4, waiting for transfers between devices, gather_tokens(): return lax.all_gather(values, 'fsdp', axis=0, tiled=True)  129 us
    all_to_all x3, blocking collectives, exchange(): lax.all_to_all(values, 'ctx', split_axis=0, concat_axis=0, tiled=True)  108 us
    all_gather x1, waiting for transfers between devices, local(): lax.all_gather(weight_gateup.astype(jnp.bfloat16), 'ctx', axis=0, tiled=T...  104 us
    reduce_scatter x4, waiting for transfers between devices, scatter_grad(): lax.psum_scatter(grad_value.astype(jnp.bfloat16), 'ctx', scatter_dimensio...  98.6 us
    reduce_scatter x4, waiting for transfers between devices, scatter_tokens(): lax.psum_scatter(partial_rows.astype(jnp.bfloat16), 'fsdp', scatter_dimen...  90.4 us
    all_gather x1, waiting for transfers between devices, local(): lax.all_gather(weight_project.astype(jnp.bfloat16), 'ctx', axis=0, tiled=...  67.3 us
    all_gather x1, waiting for transfers between devices, local(): lax.all_gather(weight_down.astype(jnp.bfloat16), 'ctx', axis=1, tiled=True)  63 us
    all_to_all x1, waiting for transfers between devices, exchange(): lax.all_to_all(values, 'ctx', split_axis=0, concat_axis=0, tiled=True)  52.9 us
  transfers between devices with their start and end apart: 17, of which 13 were waited for; matrix products, arithmetic and copies ran while one was open for 14% of the time, Pallas kernels for 6%

profile of v1, /device:TPU:0, one launch (start us, length us, event | category | flops | bytes accessed | tf_op | source)
XLA Modules:
  0.0 1092.8 jit_solution(2983441002669549619)
XLA Ops:
  10.9 15.8 %all-gather = bf16[8,1,1216]{2,1,0:T(2,128)(2,1)S(1)} all-gather(bf16[1,1,1216]{2,1,0:T(2,128)(2,1)S(1)} %bitcast.140), channel_id=1, replica_groups=mesh['ctx'=8,'fsdp'=4] {'ctx'}, dimensions={0}, use_global_device_ids=true | all-gather | bytes 21888 | tf_op jit(solution)/shard_map/all_gather | solution.py:490
  33.9 33.3 %all-gather.10.cloned.1.call-done = bf16[512,2048]{1,0:T(8,128)(2,1)} async-done(((bf16[128,2048]{1,0:T(8,128)(2,1)}), bf16[512,2048]{1,0:T(8,128)(2,1)}) %all-gather.10.cloned.1.call-update) | async-done | bytes 2097168 | tf_op jit(solution)/shard_map/all_gather | solution.py:470
  67.2 67.3 %all-gather.12.cloned.1.call-done = bf16[2048,3,512]{0,2,1:T(8,128)(2,1)} async-done(((bf16[256,3,512]{0,2,1:T(8,128)(2,1)}), bf16[2048,3,512]{0,2,1:T(8,128)(2,1)}) %all-gather.12.cloned.1.call-update) | async-done | bytes 6291472 | tf_op jit(solution)/shard_map/all_gather | solution.py:543
  134.6 6.2 fusion.7
  145.4 2.8 maximum_bitcast_fusion
  149.6 3.7 all-to-all-start
  155.0 52.9 %all-to-all-done = bf16[8,2,192,256]{3,2,1,0:T(8,128)(2,1)S(1)} async-done(((bf16[8,2,192,256]{3,2,1,0:T(8,128)(2,1)}), bf16[8,2,192,256]{3,2,1,0:T(8,128)(2,1)S(1)}, u32[]{:S(2)}, u32[]{:S(2)}) %all-to-all-start) | async-done | bytes 1572896 | tf_op jit(solution)/shard_map/all_to_all | solution.py:359
  207.9 26.9 %attend_forward.1 = (bf16[16,64,256]{2,1,0:T(8,128)(2,1)S(1)}, f32[16,64,256]{2,1,0:T(8,128)S(1)}, f32[8,1,512]{2,1,0:T(1,128)S(1)}) custom-call(s32[16]{0:T(128)S(1)} %and_select_fusion.blk_ref, bf16[16,192,256]{2,1,0:T(8,128)(2,1)S(1)} %bitcast.111), custom_call_target="tpu_custom_call" | custom-call | flops 2415919104 | bytes 3145728 | tf_op jit(solution)/shard_map/attend_forward/pallas_call | solution.py:315
  235.8 17.7 %all_to_all.20 = bf16[8,2,64,256]{3,1,2,0:T(2,128)(2,1)S(1)} all-to-all(bf16[8,2,64,256]{3,1,2,0:T(2,128)(2,1)S(1)} %copy.165), channel_id=1, replica_groups=mesh['ctx'=8,'fsdp'=4] {'ctx'}, dimensions={0} | all-to-all | bytes 1048576 | tf_op jit(solution)/shard_map/all_to_all | solution.py:359
  253.6 4.4 convolution_convert_fusion.4
  258.1 3.1 copy.213
  262.4 29.8 %reduce-scatter.10.cloned.1.call-done = bf16[128,2048]{1,0:T(8,128)(2,1)} async-done(((bf16[512,2048]{1,0:T(8,128)(2,1)}), bf16[128,2048]{1,0:T(8,128)(2,1)}) %reduce-scatter.10.cloned.1.call-update) | async-done | bytes 524304 | tf_op jit(solution)/shard_map/reduce_scatter | solution.py:474
  298.8 103.5 %all-gather.18.cloned.1.call-done = bf16[2048,2,1408]{2,0,1:T(8,128)(2,1)} async-done(((bf16[256,2,1408]{2,0,1:T(8,128)(2,1)}), bf16[2048,2,1408]{2,0,1:T(8,128)(2,1)}) %all-gather.18.cloned.1.call-update) | async-done | bytes 11534352 | tf_op jit(solution)/shard_map/all_gather | solution.py:545
  402.3 35.7 %all-gather.16.cloned.1.call-done = bf16[512,2048]{1,0:T(8,128)(2,1)} async-done(((bf16[128,2048]{1,0:T(8,128)(2,1)}), bf16[512,2048]{1,0:T(8,128)(2,1)}) %all-gather.16.cloned.1.call-update) | async-done | bytes 2097168 | tf_op jit(solution)/shard_map/all_gather | solution.py:470
  438.1 8.4 fusion.1
  446.5 5.0 fusion
  451.5 24.2 %all-gather.22.cloned.1.call-done = bf16[512,2048]{1,0:T(8,128)(2,1)} async-done(((bf16[128,2048]{1,0:T(8,128)(2,1)}), bf16[512,2048]{1,0:T(8,128)(2,1)}) %all-gather.22.cloned.1.call-update) | async-done | bytes 2097168 | tf_op jit(solution)/shard_map/all_gather | solution.py:470
  475.7 63.0 %all-gather.20.cloned.1.call-done = bf16[1408,2048]{1,0:T(8,128)(2,1)} async-done(((bf16[1408,256]{1,0:T(8,128)(2,1)}), bf16[1408,2048]{1,0:T(8,128)(2,1)}) %all-gather.20.cloned.1.call-update) | async-done | bytes 5767184 | tf_op jit(solution)/shard_map/all_gather | solution.py:546
  538.7 10.4 fusion.18
  550.6 10.0 bitcast_convert_fusion.1
  561.1 7.8 convolution_convert_fusion.5
  569.0 25.2 %reduce-scatter.14.cloned.1.call-done = bf16[128,2048]{1,0:T(8,128)(2,1)} async-done(((bf16[512,2048]{1,0:T(8,128)(2,1)}), bf16[128,2048]{1,0:T(8,128)(2,1)}) %reduce-scatter.14.cloned.1.call-update) | async-done | bytes 524304 | tf_op jit(solution)/shard_map/reduce_scatter | solution.py:474
  597.3 35.4 %reduce-scatter.12.cloned.1.call-done = bf16[128,2048]{1,0:T(8,128)(2,1)} async-done(((bf16[512,2048]{1,0:T(8,128)(2,1)}), bf16[128,2048]{1,0:T(8,128)(2,1)}) %reduce-scatter.12.cloned.1.call-update) | async-done | bytes 524304 | tf_op jit(solution)/shard_map/reduce_scatter | solution.py:474
  632.8 3.7 fusion.51
  636.5 35.3 %all-gather.24.cloned.1.call-done = bf16[512,2048]{1,0:T(8,128)(2,1)} async-done(((bf16[128,2048]{1,0:T(8,128)(2,1)}), bf16[512,2048]{1,0:T(8,128)(2,1)}) %all-gather.24.cloned.1.call-update) | async-done | bytes 2097168 | tf_op jit(solution)/shard_map/all_gather | solution.py:470
  671.8 4.3 convolution_convert_fusion.3
  676.2 7.7 convolution_convert_fusion.1
  684.0 3.5 fusion.19
  687.9 28.2 %all_to_all.21 = bf16[8,2,64,256]{3,1,2,0:T(2,128)(2,1)S(1)} all-to-all(bf16[8,2,64,256]{3,1,2,0:T(2,128)(2,1)S(1)} %bitcast.118), channel_id=1, replica_groups=mesh['ctx'=8,'fsdp'=4] {'ctx'}, dimensions={0} | all-to-all | bytes 1048576 | tf_op jit(solution)/shard_map/all_to_all | solution.py:359
  717.0 35.4 %attend_backward.1 = bf16[16,192,256]{2,1,0:T(8,128)(2,1)} custom-call(s32[16]{0:T(128)} %copy-done.1, bf16[16,192,256]{2,1,0:T(8,128)(2,1)} %bitcast.112, bf16[16,64,256]{2,1,0:T(8,128)(2,1)} %bitcast.124, f32[16,64,256]{2,1,0:T(8,128)} %copy-done.2, f32[8,1,512]{2,1,0:T(1,128)} %copy-done.3), custom_call_target="tpu_custom_call" | custom-call | flops 6039797760 | bytes 4718592 | tf_op jit(solution)/shard_map/attend_backward/pallas_call | solution.py:327
  752.4 62.1 %all_to_all.22 = bf16[8,2,192,256]{3,2,1,0:T(8,128)(2,1)S(1)} all-to-all(bf16[8,2,192,256]{3,2,1,0:T(8,128)(2,1)} %bitcast.121), channel_id=1, replica_groups=mesh['ctx'=8,'fsdp'=4] {'ctx'}, dimensions={0} | all-to-all | bytes 3145728 | tf_op jit(solution)/shard_map/all_to_all | solution.py:359
  825.1 3.0 squeeze.35
  829.3 3.0 copy.169
  832.3 3.0 squeeze.34
  845.9 8.0 bitcast_convert_fusion
  854.0 11.1 %convolution_convert_fusion = bf16[2048,2,1408]{2,0,1:T(8,128)(2,1)} fusion(bf16[512,2048]{1,0:T(8,128)(2,1)} %all-gather.16.cloned.1.call-done, bf16[1,512,1408]{2,1,0:T(8,128)(2,1)} %copy-done.53, bf16[1,512,1408]{2,1,0:T(8,128)(2,1)} %copy-done.52), kind=kOutput, calls=%fused_computation | convolution fusion | flops 5917114368 | bytes 16515072 | tf_op jit(solution)/shard_map/td,gtu->dgu/dot_general | solution.py:583
  865.4 8.2 convolution_convert_fusion.2
  880.4 26.8 %all-reduce = f32[3,8,64]{2,1,0:T(8,128)S(1)} all-reduce(f32[3,8,64]{2,1,0:T(8,128)S(1)} %convert_reduce_fusion), channel_id=7, replica_groups=mesh['ctx'=8,'fsdp'=4] {'ctx'}, use_global_device_ids=true, to_apply=%region_19.20.clone | all-reduce | flops 1536 | bytes 12288
  911.6 5.0 multiply_subtract_fusion.2
  918.3 39.4 %psum.7 = f32[4,2048]{1,0:T(4,128)S(1)} all-reduce(f32[4,2048]{1,0:T(4,128)S(1)} %pad_maximum_fusion.8), channel_id=1, replica_groups=mesh['ctx'=8,'fsdp'=4] {'ctx','fsdp'}, use_global_device_ids=true, to_apply=%region_16.17 | all-reduce | flops 8192 | bytes 65536 | tf_op jit(solution)/shard_map/psum | solution.py:616
  961.8 48.6 %reduce-scatter.22.cloned.1.call-done = bf16[256,2,1408]{2,0,1:T(8,128)(2,1)} async-done(((bf16[2048,2,1408]{2,0,1:T(8,128)(2,1)}), bf16[256,2,1408]{2,0,1:T(8,128)(2,1)}) %reduce-scatter.22.cloned.1.call-update) | async-done | bytes 1441808 | tf_op jit(solution)/shard_map/reduce_scatter | solution.py:481
  1010.4 5.5 multiply_subtract_fusion
  1016.0 3.8 copy.185
  1019.8 3.8 copy.186
  1023.6 3.8 copy.187
  1027.4 3.1 copy.184
  1030.4 50.0 %reduce-scatter.18.cloned.1.call-done = bf16[256,3,512]{2,0,1:T(8,128)(2,1)} async-done(((bf16[2048,3,512]{2,0,1:T(8,128)(2,1)}), bf16[256,3,512]{2,0,1:T(8,128)(2,1)}) %reduce-scatter.18.cloned.1.call-update) | async-done | bytes 786448 | tf_op jit(solution)/shard_map/reduce_scatter | solution.py:481
  1080.5 5.3 multiply_subtract_fusion.1
  (234 shorter events, 72.5 us)
Async XLA Ops:
  7.2 22.6 %copy-start.4 = (f32[128,2048]{1,0:T(8,128)S(1)}, f32[128,2048]{1,0:T(8,128)}, u32[]{:S(2)}) copy-start(f32[128,2048]{1,0:T(8,128)} %param.30) | copy-start | bytes 3145732
  7.2 60.0 %all-gather.10.cloned.1.call-start = ((), (), s32[]{:S(2)}) async-start(), calls=%async_computation.12 | async-start | bytes 2621440 | tf_op jit(solution)/shard_map/all_gather | solution.py:470
  30.9 103.7 %all-gather.12.cloned.1.call-start = ((), (), s32[]{:S(2)}) async-start(), calls=%async_computation.13 | async-start | bytes 7077888 | tf_op jit(solution)/shard_map/all_gather | solution.py:543
  149.6 58.3 %all-to-all-start = ((bf16[8,2,192,256]{3,2,1,0:T(8,128)(2,1)}), bf16[8,2,192,256]{3,2,1,0:T(8,128)(2,1)S(1)}, u32[]{:S(2)}, u32[]{:S(2)}) async-start(bf16[8,2,192,256]{3,2,1,0:T(8,128)(2,1)} %bitcast.114), calls=%async_computation | async-start | bytes 3145728 | tf_op jit(solution)/shard_map/all_to_all | solution.py:359
  153.3 100.3 %all-gather.14.cloned.1.call-start = ((), (), s32[]{:S(2)}) async-start(), calls=%async_computation.14 | async-start | bytes 2359296 | tf_op jit(solution)/shard_map/all_gather | solution.py:544
  154.1 138.1 %reduce-scatter.10.cloned.1.call-start = ((), (), s32[]{:S(2)}) async-start(), calls=%async_computation.15 | async-start | bytes 2621440 | tf_op jit(solution)/shard_map/reduce_scatter | solution.py:474
  155.0 79.8 %copy-start.1 = (s32[16]{0:T(128)}, s32[16]{0:T(128)S(1)}, u32[]{:S(2)}) copy-start(s32[16]{0:T(128)S(1)} %and_select_fusion.blk_ref) | copy-start | bytes 196
  207.9 26.9 %copy-start = (bf16[8,2,192,256]{3,2,1,0:T(8,128)(2,1)}, bf16[8,2,192,256]{3,2,1,0:T(8,128)(2,1)S(1)}, u32[]{:S(2)}) copy-start(bf16[8,2,192,256]{3,2,1,0:T(8,128)(2,1)S(1)} %all-to-all-done) | copy-start | bytes 4718596
  234.8 18.7 %copy-start.3 = (f32[8,1,512]{2,1,0:T(1,128)}, f32[8,1,512]{2,1,0:T(1,128)S(1)}, u32[]{:S(2)}) copy-start(f32[8,1,512]{2,1,0:T(1,128)S(1)} %get-tuple-element.43.lse_ref) | copy-start | bytes 49156
  258.0 144.3 %all-gather.18.cloned.1.call-start = ((), (), s32[]{:S(2)}) async-start(), calls=%async_computation.17 | async-start | bytes 12976128 | tf_op jit(solution)/shard_map/all_gather | solution.py:545
  261.2 176.9 %all-gather.16.cloned.1.call-start = ((), (), s32[]{:S(2)}) async-start(), calls=%async_computation.16 | async-start | bytes 2621440 | tf_op jit(solution)/shard_map/all_gather | solution.py:470
  295.4 180.3 %all-gather.22.cloned.1.call-start = ((), (), s32[]{:S(2)}) async-start(), calls=%async_computation.20 | async-start | bytes 2621440 | tf_op jit(solution)/shard_map/all_gather | solution.py:470
  297.5 241.2 %all-gather.20.cloned.1.call-start = ((), (), s32[]{:S(2)}) async-start(), calls=%async_computation.18 | async-start | bytes 6488064 | tf_op jit(solution)/shard_map/all_gather | solution.py:546
  298.5 295.6 %reduce-scatter.14.cloned.1.call-start = ((), (), s32[]{:S(2)}) async-start(), calls=%async_computation.21 | async-start | bytes 2621440 | tf_op jit(solution)/shard_map/reduce_scatter | solution.py:474
  438.1 8.4 copy-start.49
  438.1 8.4 copy-start.50
  560.7 72.1 %reduce-scatter.12.cloned.1.call-start = ((), (), s32[]{:S(2)}) async-start(), calls=%async_computation.19 | async-start | bytes 2621440 | tf_op jit(solution)/shard_map/reduce_scatter | solution.py:474
  569.0 102.9 %all-gather.24.cloned.1.call-start = ((), (), s32[]{:S(2)}) async-start(), calls=%async_computation.22 | async-start | bytes 2621440 | tf_op jit(solution)/shard_map/all_gather | solution.py:470
  636.5 272.2 %reduce-scatter.20.cloned.1.call-start = ((), (), s32[]{:S(2)}) async-start(), calls=%async_computation.25 | async-start | bytes 2359296 | tf_op jit(solution)/shard_map/reduce_scatter | solution.py:481
  676.2 235.4 %reduce-scatter.24.cloned.1.call-start = ((), (), s32[]{:S(2)}) async-start(), calls=%async_computation.27 | async-start | bytes 6488064 | tf_op jit(solution)/shard_map/reduce_scatter | solution.py:481
  684.0 232.6 %reduce-scatter.16.cloned.1.call-start = ((), (), s32[]{:S(2)}) async-start(), calls=%async_computation.23 | async-start | bytes 2621440 | tf_op jit(solution)/shard_map/reduce_scatter | solution.py:474
  853.9 156.5 %reduce-scatter.22.cloned.1.call-start = ((), (), s32[]{:S(2)}) async-start(), calls=%async_computation.26 | async-start | bytes 12976128 | tf_op jit(solution)/shard_map/reduce_scatter | solution.py:481
  865.1 215.3 %reduce-scatter.18.cloned.1.call-start = ((), (), s32[]{:S(2)}) async-start(), calls=%async_computation.24 | async-start | bytes 7077888 | tf_op jit(solution)/shard_map/reduce_scatter | solution.py:481
  879.0 28.2 %copy-start.23 = (f32[3,8,8]{2,1,0:T(8,128)S(1)}, f32[3,8,8]{2,1,0:T(8,128)}, u32[]{:S(2)}) copy-start(f32[3,8,8]{2,1,0:T(8,128)} %param.36) | copy-start | bytes 2308
  880.0 28.7 %copy-start.13 = (f32[512,256]{1,0:T(8,128)S(1)}, f32[512,256]{1,0:T(8,128)}, u32[]{:S(2)}) copy-start(f32[512,256]{1,0:T(8,128)} %param.37) | copy-start | bytes 1572868
  911.4 5.2 copy-start.28
  911.4 5.2 copy-start.31
  911.4 6.9 copy-start.25
  911.4 6.8 copy-start.26
  911.4 46.4 %copy-start.37 = (f32[256]{0:T(256)S(1)}, f32[256]{0:T(256)}, u32[]{:S(2)}) copy-start(f32[256]{0:T(256)} %param.33) | copy-start | bytes 3076
  911.4 46.4 %copy-start.38 = (f32[256]{0:T(256)S(1)}, f32[256]{0:T(256)}, u32[]{:S(2)}) copy-start(f32[256]{0:T(256)} %param.42) | copy-start | bytes 3076
  911.5 46.4 %copy-start.39 = (f32[256]{0:T(256)S(1)}, f32[256]{0:T(256)}, u32[]{:S(2)}) copy-start(f32[256]{0:T(256)} %param.51) | copy-start | bytes 3076
  911.5 47.0 %copy-start.40 = (f32[256]{0:T(256)S(1)}, f32[256]{0:T(256)}, u32[]{:S(2)}) copy-start(f32[256]{0:T(256)} %param.34) | copy-start | bytes 3076
  911.5 47.0 %copy-start.41 = (f32[256]{0:T(256)S(1)}, f32[256]{0:T(256)}, u32[]{:S(2)}) copy-start(f32[256]{0:T(256)} %param.43) | copy-start | bytes 3076
  911.5 47.0 %copy-start.42 = (f32[256]{0:T(256)S(1)}, f32[256]{0:T(256)}, u32[]{:S(2)}) copy-start(f32[256]{0:T(256)} %param.52) | copy-start | bytes 3076
  911.5 47.6 %copy-start.43 = (f32[256]{0:T(256)S(1)}, f32[256]{0:T(256)}, u32[]{:S(2)}) copy-start(f32[256]{0:T(256)} %param.38) | copy-start | bytes 3076
  911.5 47.6 %copy-start.44 = (f32[256]{0:T(256)S(1)}, f32[256]{0:T(256)}, u32[]{:S(2)}) copy-start(f32[256]{0:T(256)} %param.47) | copy-start | bytes 3076
  911.5 47.6 %copy-start.45 = (f32[256]{0:T(256)S(1)}, f32[256]{0:T(256)}, u32[]{:S(2)}) copy-start(f32[256]{0:T(256)} %param.56) | copy-start | bytes 3076
  911.5 48.2 %copy-start.46 = (f32[256]{0:T(256)S(1)}, f32[256]{0:T(256)}, u32[]{:S(2)}) copy-start(f32[256]{0:T(256)} %param.39) | copy-start | bytes 3076
  911.6 48.1 %copy-start.47 = (f32[256]{0:T(256)S(1)}, f32[256]{0:T(256)}, u32[]{:S(2)}) copy-start(f32[256]{0:T(256)} %param.48) | copy-start | bytes 3076
  911.6 48.1 %copy-start.48 = (f32[256]{0:T(256)S(1)}, f32[256]{0:T(256)}, u32[]{:S(2)}) copy-start(f32[256]{0:T(256)} %param.57) | copy-start | bytes 3076
  916.6 43.7 %copy-start.10 = (f32[128,2048]{1,0:T(8,128)S(1)}, f32[128,2048]{1,0:T(8,128)}, u32[]{:S(2)}) copy-start(f32[128,2048]{1,0:T(8,128)} %get-tuple-element.274) | copy-start | bytes 3145732
  916.6 43.7 %copy-start.14 = (bf16[128,2048]{1,0:T(8,128)(2,1)S(1)}, bf16[128,2048]{1,0:T(8,128)(2,1)}, u32[]{:S(2)}) copy-start(bf16[128,2048]{1,0:T(8,128)(2,1)} %reduce-scatter.16.cloned.1.call-done) | copy-start | bytes 1572868
  957.8 58.1 %copy-start.33 = (f32[1,256]{1,0:T(1,128)}, f32[1,256]{1,0:T(1,128)S(1)}, u32[]{:S(2)}) copy-start(f32[1,256]{1,0:T(1,128)S(1)} %get-tuple-element.293) | copy-start | bytes 3076
  957.8 58.1 %copy-start.34 = (f32[1,256]{1,0:T(1,128)}, f32[1,256]{1,0:T(1,128)S(1)}, u32[]{:S(2)}) copy-start(f32[1,256]{1,0:T(1,128)S(1)} %get-tuple-element.294) | copy-start | bytes 3076
  957.8 58.1 %copy-start.35 = (f32[1,256]{1,0:T(1,128)}, f32[1,256]{1,0:T(1,128)S(1)}, u32[]{:S(2)}) copy-start(f32[1,256]{1,0:T(1,128)S(1)} %get-tuple-element.295) | copy-start | bytes 3076
  957.8 58.1 %copy-start.36 = (f32[1,256]{1,0:T(1,128)}, f32[1,256]{1,0:T(1,128)S(1)}, u32[]{:S(2)}) copy-start(f32[1,256]{1,0:T(1,128)S(1)} %get-tuple-element.296) | copy-start | bytes 3076
  1027.4 53.1 %copy-start.7 = (f32[256,3,512]{2,0,1:T(8,128)S(1)}, f32[256,3,512]{2,0,1:T(8,128)}, u32[]{:S(2)}) copy-start(f32[256,3,512]{2,0,1:T(8,128)} %param.35) | copy-start | bytes 4718596
  (23 other events, 53.4 us)
Sparse Core Ops, SparseCore 0:
  31.0 36.2 all-gather.9
  69.4 65.1 all-gather.11
  156.3 51.3 all-gather.13
  258.1 34.0 reduce-scatter.9
  294.3 108.0 all-gather.17
  404.6 33.4 all-gather.15
  440.5 35.1 all-gather.21
  477.9 60.8 all-gather.19
  560.8 33.3 reduce-scatter.13
  597.6 35.1 reduce-scatter.11
  636.6 35.1 all-gather.23
  676.3 40.2 reduce-scatter.19
  718.9 89.0 reduce-scatter.23
  854.1 33.6 reduce-scatter.15
  889.9 120.4 reduce-scatter.21
  1012.6 67.8 reduce-scatter.17
